TPU v7x, 512 devices: a whole 4x8x8 slice. The times are simulated.
512 devices in a mesh: los: 32 (over z, x), sky: 16 (over y, core).
Axes of the slice: x: 4, y: 8, z: 8, core: 2. Of those that a mesh axis runs over, the one named last changes fastest.
Arguments:
- part_cell: int32 [3, 2097152], P(None, ('los', 'sky')), may hold values from 0 to 127, as said below
- part_frac: float32 [3, 2097152], P(None, ('los', 'sky')), may hold values from 0 to 1
- los_offset: int32 [2097152], P(('los', 'sky')), may hold values from -32 to 32
- block_dest: int32 [16384], P(('los', 'sky')), may hold values from 0 to 31, as said below
- block_count: int32 [16384], P(('los', 'sky')), may hold values from 96 to 128, as said below
- selection: float32 [128, 64, 128], P('los', 'sky'), may hold values from 0.3 to 3
- galaxy_counts: int32 [128, 64, 128], P('los', 'sky'), may hold values from 0 to 5
- bias_exp: float32 [128], P('los'), may hold values from 1.2 to 2.2
- rsd_factor: float32 [128], P('los'), may hold values from 0.5 to 2
Outputs:
- grad_pos: float32 [3, 2097152], P(None, ('los', 'sky'))
- grad_vel: float32 [2097152], P(('los', 'sky'))
Inputs may be any that keep to these rules, and one draw needn't show every extreme that they name: Component 1 of a particle lies in the first-sky cells of its own device's columns, and (part_cell[0] + los_offset) mod 128 lies in cells block_dest * 4 to block_dest * 4 + 3 of the particle's block, for every slot. `block_dest`: the 32 blocks of one device name any slab at most 2 times, and on every device some slab is named exactly 2 times. `block_count`: A block's live particles are its first slots; every device has a full block.
All inputs are finite; a program needn't handle non-finite values.
Results may differ from a plain program's by a relative error of at most 0.000098.
Values sent between devices are 32-bit elements; how exact they have to be, the bound alone decides.
A program may use at most 64 MiB of HBM per device.

v0:
```python
import jax
import jax.numpy as jnp
from jax import lax
from jax.sharding import PartitionSpec as P


def passed_along(block, axis, distance):
    devices = range(lax.axis_size(axis))
    route = [((i - distance) % len(devices), i) for i in devices]
    return lax.ppermute(block, axis, route)


def factor(fraction, bit):
    return fraction if bit else 1.0 - fraction


def slope(bit):
    return 1.0 if bit else -1.0


def with_sky_rim(field):
    from_right = passed_along(field[:, 0], "sky", -1)
    return jnp.concatenate([field, from_right[:, None]], axis=1)


def group_tables(group_rows, plane_cols, plane_size, deep_width):
    flat_rows = group_rows.transpose(1, 0, 2).reshape(group_rows.shape[1], -1)
    los_here = flat_rows[0].astype(jnp.int32)
    sky_here = flat_rows[1].astype(jnp.int32)
    deep_here = flat_rows[2].astype(jnp.int32)
    frac_los = flat_rows[3]
    frac_sky = flat_rows[4]
    frac_deep = flat_rows[5]
    live_here = flat_rows[6]
    base = los_here * plane_cols + sky_here
    plane_iota = jnp.arange(plane_size, dtype=jnp.int32)[None, :]
    plane_val = jnp.zeros((base.shape[0], plane_size), jnp.float32)
    plane_los = jnp.zeros((base.shape[0], plane_size), jnp.float32)
    plane_sky = jnp.zeros((base.shape[0], plane_size), jnp.float32)
    for los_bit in (0, 1):
        for sky_bit in (0, 1):
            hit = (plane_iota == (base + los_bit * plane_cols + sky_bit)[:, None]).astype(
                jnp.float32
            )
            weight_los = factor(frac_los, los_bit)
            weight_sky = factor(frac_sky, sky_bit)
            plane_val = plane_val + (weight_los * weight_sky)[:, None] * hit
            plane_los = plane_los + (slope(los_bit) * weight_sky)[:, None] * hit
            plane_sky = plane_sky + (weight_los * slope(sky_bit))[:, None] * hit
    deep_iota = jnp.arange(deep_width, dtype=jnp.int32)[None, :]
    lower = deep_iota == deep_here[:, None]
    upper = deep_iota == jnp.mod(deep_here + 1, deep_width)[:, None]
    deep_val = jnp.where(lower, 1.0 - frac_deep[:, None], 0.0) + jnp.where(
        upper, frac_deep[:, None], 0.0
    )
    deep_slope = upper.astype(jnp.float32) - lower.astype(jnp.float32)
    return (plane_val, plane_los, plane_sky, deep_val, deep_slope, live_here)


def on_device(
    part_cell,
    part_frac,
    los_offset,
    block_dest,
    block_count,
    selection,
    galaxy_counts,
    bias_exp,
    rsd_factor,
):
    slab_rows, sky_width, deep_width = selection.shape
    los_devices = lax.axis_size("los")
    sky_here = lax.axis_index("sky")
    block_total = block_dest.shape[0]
    block_size = part_cell.shape[1] // block_total
    capacity = 2 * block_total // los_devices
    row_in_slab = jnp.mod(part_cell[0] + los_offset, slab_rows)
    slot_index = jnp.arange(block_size, dtype=jnp.int32)
    alive = (slot_index[None, :] < block_count[:, None]).astype(jnp.float32).reshape(-1)
    sky_local = part_cell[1] - sky_here * sky_width
    deep_cell = part_cell[2]
    located = jnp.stack(
        [
            row_in_slab.astype(jnp.float32),
            sky_local.astype(jnp.float32),
            deep_cell.astype(jnp.float32),
        ]
    )
    payload = jnp.concatenate([located, part_frac], axis=0)
    payload = payload.reshape(6, block_total, block_size).transpose(1, 0, 2)
    member = (block_dest[:, None] == jnp.arange(los_devices, dtype=jnp.int32)[None, :]).astype(
        jnp.int32
    )
    before = jnp.cumsum(member, axis=0) - member
    ranking = jnp.sum(before * member, axis=1)
    target = block_dest * capacity + ranking
    outgoing = (
        jnp.zeros((los_devices * capacity, 6, block_size), jnp.float32).at[target].set(payload)
    )
    outgoing = outgoing.reshape(los_devices, capacity, 6, block_size)
    out_counts = jnp.zeros((los_devices * capacity,), jnp.int32).at[target].set(block_count)
    out_counts = out_counts.reshape(los_devices, capacity)
    arrived, arrived_counts = (
        lax.all_to_all(outgoing, "los", split_axis=0, concat_axis=0, tiled=True),
        lax.all_to_all(out_counts, "los", split_axis=0, concat_axis=0, tiled=True),
    )
    recv_blocks = los_devices * capacity
    arrived = arrived.reshape(recv_blocks, 6, block_size)
    slot_live = (slot_index[None, :] < arrived_counts.reshape(-1)[:, None]).astype(jnp.float32)
    recv_los = arrived[:, 0].astype(jnp.int32)
    plane_rows = slab_rows + 1
    plane_cols = sky_width + 1
    plane_size = plane_rows * plane_cols
    group = 4
    group_count = recv_blocks // group
    grouped = jnp.concatenate([arrived, slot_live[:, None, :]], axis=1).reshape(
        group_count, group, 7, block_size
    )

    def deposit(painted, group_rows):
        plane_val, plane_los, plane_sky, deep_val, deep_slope, live_here = group_tables(
            group_rows, plane_cols, plane_size, deep_width
        )
        term = lax.dot_general(
            plane_val * live_here[:, None],
            deep_val,
            (((0,), (0,)), ((), ())),
            precision=lax.Precision.HIGHEST,
            preferred_element_type=jnp.float32,
        )
        return (painted + term, None)

    painted, unused = lax.scan(deposit, jnp.zeros((plane_size, deep_width), jnp.float32), grouped)
    painted = painted.reshape(plane_rows, plane_cols, deep_width)
    from_below = passed_along(painted[slab_rows], "los", 1)
    core = painted[:slab_rows].at[0].add(from_below)
    from_left = passed_along(core[:, sky_width], "sky", 1)
    density = core[:, :sky_width].at[:, 0].add(from_left)
    shifted = density + 0.5
    exponent = bias_exp[:, None, None]
    intensity = selection * jnp.exp(exponent * jnp.log(shifted))
    cotangent = (
        (1.0 - galaxy_counts.astype(jnp.float32) / intensity) * exponent * intensity / shifted
    )
    sky_framed = with_sky_rim(cotangent)
    from_above = passed_along(sky_framed[0], "los", -1)
    extended = jnp.concatenate([sky_framed, from_above[None]], axis=0)
    field_plane = extended.reshape(plane_size, deep_width)

    def pull(group_rows):
        plane_val, plane_los, plane_sky, deep_val, deep_slope, live_here = group_tables(
            group_rows, plane_cols, plane_size, deep_width
        )
        stacked = jnp.concatenate([plane_los, plane_sky, plane_val], axis=0)
        picked = jnp.dot(
            stacked,
            field_plane,
            precision=lax.Precision.HIGHEST,
            preferred_element_type=jnp.float32,
        )
        picked = picked.reshape(3, -1, deep_width)
        sum_los = jnp.sum(picked[0] * deep_val, axis=1)
        sum_sky = jnp.sum(picked[1] * deep_val, axis=1)
        sum_deep = jnp.sum(picked[2] * deep_slope, axis=1)
        return jnp.stack([sum_los, sum_sky, sum_deep]).reshape(3, group, block_size)

    pulled = lax.map(pull, grouped)
    pulled = pulled.transpose(0, 2, 1, 3).reshape(recv_blocks, 3, block_size)
    rate_each = rsd_factor[recv_los]
    returned = (
        jnp.concatenate([pulled, (rate_each * pulled[:, 0])[:, None]], axis=1)
        * slot_live[:, None, :]
    )
    returned = returned.reshape(los_devices, capacity, 4, block_size)
    came_back = lax.all_to_all(returned, "los", split_axis=0, concat_axis=0, tiled=True)
    own_rows = came_back.reshape(los_devices * capacity, 4, block_size)[target]
    own_rows = own_rows.transpose(1, 0, 2).reshape(4, -1)
    grad_pos = own_rows[:3] * alive[None, :]
    grad_vel = own_rows[3] * alive
    return (grad_pos, grad_vel)


def solution(mesh):
    return jax.shard_map(
        on_device,
        mesh=mesh,
        in_specs=(
            P(None, ("los", "sky")),
            P(None, ("los", "sky")),
            P(("los", "sky")),
            P(("los", "sky")),
            P(("los", "sky")),
            P("los", "sky", None),
            P("los", "sky", None),
            P("los"),
            P("los"),
        ),
        out_specs=(P(None, ("los", "sky")), P(("los", "sky"))),
        check_vma=False,
    )
```

profile of v0, /device:TPU:25, one launch (start us, length us, event | category | flops | bytes accessed | tf_op | source)
XLA Modules:
  0.0 129.4 jit_solution(5884438748901623500)
XLA Ops:
  3.7 12.9 %all-to-all-start.1 = ((s32[32,1,2]{2,1,0:T(1,128)}), s32[32,1,2]{2,1,0:T(1,128)S(1)}, u32[]{:S(2)}, u32[]{:S(2)}) async-start(s32[32,1,2]{2,1,0:T(1,128)} %bitcast.21), calls=%async_computation.1 | async-start | bytes 32768 | tf_op jit(solution)/shard_map/all_to_all | solution.py:105
  17.5 1.5 %scatter_fusion = f32[64,6,128]{2,1,0:T(8,128)S(1)} fusion(f32[64,6,128]{2,1,0:T(8,128)S(1)} %broadcast_in_dim.124, s32[32]{0:T(128)S(1)} %compare_select_fusion.1, f32[32,6,128]{2,1,0:T(8,128)S(1)} %maximum_bitcast_fusion), kind=kCustom, calls=%fused_computation.1 | custom fusion | bytes 295040 | tf_op jit(solution)/shard_map/scatter | solution.py:98
  19.8 5.3 %all-to-all-done.1 = s32[32,1,2]{2,1,0:T(1,128)S(1)} async-done(((s32[32,1,2]{2,1,0:T(1,128)}), s32[32,1,2]{2,1,0:T(1,128)S(1)}, u32[]{:S(2)}, u32[]{:S(2)}) %all-to-all-start.1) | async-done | bytes 288 | tf_op jit(solution)/shard_map/all_to_all | solution.py:105
  25.1 3.9 %all-to-all-start = ((f32[32,2,6,128]{3,1,2,0:T(2,128)}), f32[32,2,6,128]{3,1,2,0:T(2,128)S(1)}, u32[]{:S(2)}, u32[]{:S(2)}) async-start(f32[32,2,6,128]{3,1,2,0:T(2,128)} %copy.52), calls=%async_computation | async-start | bytes 393216 | tf_op jit(solution)/shard_map/all_to_all | solution.py:104
  30.4 8.5 %all-to-all-done = f32[32,2,6,128]{3,1,2,0:T(2,128)S(1)} async-done(((f32[32,2,6,128]{3,1,2,0:T(2,128)}), f32[32,2,6,128]{3,1,2,0:T(2,128)S(1)}, u32[]{:S(2)}, u32[]{:S(2)}) %all-to-all-start) | async-done | bytes 196640 | tf_op jit(solution)/shard_map/all_to_all | solution.py:104
  39.2 26.2 %while.28 = (s32[]{:T(128)}, f32[25,128]{1,0:T(8,128)S(1)}, f32[16,4,7,128]{3,2,1,0:T(8,128)S(1)}, s32[]{:T(128)}, s32[]{:T(128)}) while((s32[]{:T(128)}, f32[25,128]{1,0:T(8,128)S(1)}, f32[16,4,7,128]{3,2,1,0:T(8,128)S(1)}, s32[]{:T(128)}, s32[]{:T(128)}) %tuple.116), condition=%wide.region_5.6_spmd.clone, body=%wide.region_4.5_spmd.clone.sunk | while | flops 20162308 | bytes 136267 | solution.py:133
  39.3 1.5 %convolution_add_fusion.2 = f32[25,128]{1,0:T(8,128)S(1)} fusion(f32[512]{0:T(512)S(1)} %bitcast.144, s32[512]{0:T(512)S(1)} %get-tuple-element.311, f32[512]{0:T(512)S(1)} %get-tuple-element.314, s32[512]{0:T(512)S(1)} %bitcast.140, f32[512]{0:T(512)S(1)} %bitcast.154, f32[512]{0:T(512)S(1)} %get-tuple-element.316, s32[512]{0:T(512)S(1)} %get-tuple-element.317, ...), kind=kOutput, calls=%fused_computation.50.clone.1 | convolution fusion | flops 20148480 | bytes 52225 | tf_op jit(solution)/shard_map/while/body/eval_jaxpr/dot_general | solution.py:124
  40.9 1.5 %convolution_add_fusion.2 = f32[25,128]{1,0:T(8,128)S(1)} fusion(f32[512]{0:T(512)S(1)} %bitcast.144, s32[512]{0:T(512)S(1)} %get-tuple-element.311, f32[512]{0:T(512)S(1)} %get-tuple-element.314, s32[512]{0:T(512)S(1)} %bitcast.140, f32[512]{0:T(512)S(1)} %bitcast.154, f32[512]{0:T(512)S(1)} %get-tuple-element.316, s32[512]{0:T(512)S(1)} %get-tuple-element.317, ...), kind=kOutput, calls=%fused_computation.50.clone.1 | convolution fusion | flops 20148480 | bytes 52225 | tf_op jit(solution)/shard_map/while/body/eval_jaxpr/dot_general | solution.py:124
  42.6 1.5 %convolution_add_fusion.2 = f32[25,128]{1,0:T(8,128)S(1)} fusion(f32[512]{0:T(512)S(1)} %bitcast.144, s32[512]{0:T(512)S(1)} %get-tuple-element.311, f32[512]{0:T(512)S(1)} %get-tuple-element.314, s32[512]{0:T(512)S(1)} %bitcast.140, f32[512]{0:T(512)S(1)} %bitcast.154, f32[512]{0:T(512)S(1)} %get-tuple-element.316, s32[512]{0:T(512)S(1)} %get-tuple-element.317, ...), kind=kOutput, calls=%fused_computation.50.clone.1 | convolution fusion | flops 20148480 | bytes 52225 | tf_op jit(solution)/shard_map/while/body/eval_jaxpr/dot_general | solution.py:124
  44.2 1.5 %convolution_add_fusion.2 = f32[25,128]{1,0:T(8,128)S(1)} fusion(f32[512]{0:T(512)S(1)} %bitcast.144, s32[512]{0:T(512)S(1)} %get-tuple-element.311, f32[512]{0:T(512)S(1)} %get-tuple-element.314, s32[512]{0:T(512)S(1)} %bitcast.140, f32[512]{0:T(512)S(1)} %bitcast.154, f32[512]{0:T(512)S(1)} %get-tuple-element.316, s32[512]{0:T(512)S(1)} %get-tuple-element.317, ...), kind=kOutput, calls=%fused_computation.50.clone.1 | convolution fusion | flops 20148480 | bytes 52225 | tf_op jit(solution)/shard_map/while/body/eval_jaxpr/dot_general | solution.py:124
  45.8 1.5 %convolution_add_fusion.2 = f32[25,128]{1,0:T(8,128)S(1)} fusion(f32[512]{0:T(512)S(1)} %bitcast.144, s32[512]{0:T(512)S(1)} %get-tuple-element.311, f32[512]{0:T(512)S(1)} %get-tuple-element.314, s32[512]{0:T(512)S(1)} %bitcast.140, f32[512]{0:T(512)S(1)} %bitcast.154, f32[512]{0:T(512)S(1)} %get-tuple-element.316, s32[512]{0:T(512)S(1)} %get-tuple-element.317, ...), kind=kOutput, calls=%fused_computation.50.clone.1 | convolution fusion | flops 20148480 | bytes 52225 | tf_op jit(solution)/shard_map/while/body/eval_jaxpr/dot_general | solution.py:124
  47.5 1.5 %convolution_add_fusion.2 = f32[25,128]{1,0:T(8,128)S(1)} fusion(f32[512]{0:T(512)S(1)} %bitcast.144, s32[512]{0:T(512)S(1)} %get-tuple-element.311, f32[512]{0:T(512)S(1)} %get-tuple-element.314, s32[512]{0:T(512)S(1)} %bitcast.140, f32[512]{0:T(512)S(1)} %bitcast.154, f32[512]{0:T(512)S(1)} %get-tuple-element.316, s32[512]{0:T(512)S(1)} %get-tuple-element.317, ...), kind=kOutput, calls=%fused_computation.50.clone.1 | convolution fusion | flops 20148480 | bytes 52225 | tf_op jit(solution)/shard_map/while/body/eval_jaxpr/dot_general | solution.py:124
  49.1 1.5 %convolution_add_fusion.2 = f32[25,128]{1,0:T(8,128)S(1)} fusion(f32[512]{0:T(512)S(1)} %bitcast.144, s32[512]{0:T(512)S(1)} %get-tuple-element.311, f32[512]{0:T(512)S(1)} %get-tuple-element.314, s32[512]{0:T(512)S(1)} %bitcast.140, f32[512]{0:T(512)S(1)} %bitcast.154, f32[512]{0:T(512)S(1)} %get-tuple-element.316, s32[512]{0:T(512)S(1)} %get-tuple-element.317, ...), kind=kOutput, calls=%fused_computation.50.clone.1 | convolution fusion | flops 20148480 | bytes 52225 | tf_op jit(solution)/shard_map/while/body/eval_jaxpr/dot_general | solution.py:124
  50.8 1.5 %convolution_add_fusion.2 = f32[25,128]{1,0:T(8,128)S(1)} fusion(f32[512]{0:T(512)S(1)} %bitcast.144, s32[512]{0:T(512)S(1)} %get-tuple-element.311, f32[512]{0:T(512)S(1)} %get-tuple-element.314, s32[512]{0:T(512)S(1)} %bitcast.140, f32[512]{0:T(512)S(1)} %bitcast.154, f32[512]{0:T(512)S(1)} %get-tuple-element.316, s32[512]{0:T(512)S(1)} %get-tuple-element.317, ...), kind=kOutput, calls=%fused_computation.50.clone.1 | convolution fusion | flops 20148480 | bytes 52225 | tf_op jit(solution)/shard_map/while/body/eval_jaxpr/dot_general | solution.py:124
  52.4 1.5 %convolution_add_fusion.2 = f32[25,128]{1,0:T(8,128)S(1)} fusion(f32[512]{0:T(512)S(1)} %bitcast.144, s32[512]{0:T(512)S(1)} %get-tuple-element.311, f32[512]{0:T(512)S(1)} %get-tuple-element.314, s32[512]{0:T(512)S(1)} %bitcast.140, f32[512]{0:T(512)S(1)} %bitcast.154, f32[512]{0:T(512)S(1)} %get-tuple-element.316, s32[512]{0:T(512)S(1)} %get-tuple-element.317, ...), kind=kOutput, calls=%fused_computation.50.clone.1 | convolution fusion | flops 20148480 | bytes 52225 | tf_op jit(solution)/shard_map/while/body/eval_jaxpr/dot_general | solution.py:124
  54.0 1.5 %convolution_add_fusion.2 = f32[25,128]{1,0:T(8,128)S(1)} fusion(f32[512]{0:T(512)S(1)} %bitcast.144, s32[512]{0:T(512)S(1)} %get-tuple-element.311, f32[512]{0:T(512)S(1)} %get-tuple-element.314, s32[512]{0:T(512)S(1)} %bitcast.140, f32[512]{0:T(512)S(1)} %bitcast.154, f32[512]{0:T(512)S(1)} %get-tuple-element.316, s32[512]{0:T(512)S(1)} %get-tuple-element.317, ...), kind=kOutput, calls=%fused_computation.50.clone.1 | convolution fusion | flops 20148480 | bytes 52225 | tf_op jit(solution)/shard_map/while/body/eval_jaxpr/dot_general | solution.py:124
  55.7 1.5 %convolution_add_fusion.2 = f32[25,128]{1,0:T(8,128)S(1)} fusion(f32[512]{0:T(512)S(1)} %bitcast.144, s32[512]{0:T(512)S(1)} %get-tuple-element.311, f32[512]{0:T(512)S(1)} %get-tuple-element.314, s32[512]{0:T(512)S(1)} %bitcast.140, f32[512]{0:T(512)S(1)} %bitcast.154, f32[512]{0:T(512)S(1)} %get-tuple-element.316, s32[512]{0:T(512)S(1)} %get-tuple-element.317, ...), kind=kOutput, calls=%fused_computation.50.clone.1 | convolution fusion | flops 20148480 | bytes 52225 | tf_op jit(solution)/shard_map/while/body/eval_jaxpr/dot_general | solution.py:124
  57.3 1.5 %convolution_add_fusion.2 = f32[25,128]{1,0:T(8,128)S(1)} fusion(f32[512]{0:T(512)S(1)} %bitcast.144, s32[512]{0:T(512)S(1)} %get-tuple-element.311, f32[512]{0:T(512)S(1)} %get-tuple-element.314, s32[512]{0:T(512)S(1)} %bitcast.140, f32[512]{0:T(512)S(1)} %bitcast.154, f32[512]{0:T(512)S(1)} %get-tuple-element.316, s32[512]{0:T(512)S(1)} %get-tuple-element.317, ...), kind=kOutput, calls=%fused_computation.50.clone.1 | convolution fusion | flops 20148480 | bytes 52225 | tf_op jit(solution)/shard_map/while/body/eval_jaxpr/dot_general | solution.py:124
  59.0 1.5 %convolution_add_fusion.2 = f32[25,128]{1,0:T(8,128)S(1)} fusion(f32[512]{0:T(512)S(1)} %bitcast.144, s32[512]{0:T(512)S(1)} %get-tuple-element.311, f32[512]{0:T(512)S(1)} %get-tuple-element.314, s32[512]{0:T(512)S(1)} %bitcast.140, f32[512]{0:T(512)S(1)} %bitcast.154, f32[512]{0:T(512)S(1)} %get-tuple-element.316, s32[512]{0:T(512)S(1)} %get-tuple-element.317, ...), kind=kOutput, calls=%fused_computation.50.clone.1 | convolution fusion | flops 20148480 | bytes 52225 | tf_op jit(solution)/shard_map/while/body/eval_jaxpr/dot_general | solution.py:124
  60.6 1.5 %convolution_add_fusion.2 = f32[25,128]{1,0:T(8,128)S(1)} fusion(f32[512]{0:T(512)S(1)} %bitcast.144, s32[512]{0:T(512)S(1)} %get-tuple-element.311, f32[512]{0:T(512)S(1)} %get-tuple-element.314, s32[512]{0:T(512)S(1)} %bitcast.140, f32[512]{0:T(512)S(1)} %bitcast.154, f32[512]{0:T(512)S(1)} %get-tuple-element.316, s32[512]{0:T(512)S(1)} %get-tuple-element.317, ...), kind=kOutput, calls=%fused_computation.50.clone.1 | convolution fusion | flops 20148480 | bytes 52225 | tf_op jit(solution)/shard_map/while/body/eval_jaxpr/dot_general | solution.py:124
  62.2 1.5 %convolution_add_fusion.2 = f32[25,128]{1,0:T(8,128)S(1)} fusion(f32[512]{0:T(512)S(1)} %bitcast.144, s32[512]{0:T(512)S(1)} %get-tuple-element.311, f32[512]{0:T(512)S(1)} %get-tuple-element.314, s32[512]{0:T(512)S(1)} %bitcast.140, f32[512]{0:T(512)S(1)} %bitcast.154, f32[512]{0:T(512)S(1)} %get-tuple-element.316, s32[512]{0:T(512)S(1)} %get-tuple-element.317, ...), kind=kOutput, calls=%fused_computation.50.clone.1 | convolution fusion | flops 20148480 | bytes 52225 | tf_op jit(solution)/shard_map/while/body/eval_jaxpr/dot_general | solution.py:124
  63.9 1.5 %convolution_add_fusion.2 = f32[25,128]{1,0:T(8,128)S(1)} fusion(f32[512]{0:T(512)S(1)} %bitcast.144, s32[512]{0:T(512)S(1)} %get-tuple-element.311, f32[512]{0:T(512)S(1)} %get-tuple-element.314, s32[512]{0:T(512)S(1)} %bitcast.140, f32[512]{0:T(512)S(1)} %bitcast.154, f32[512]{0:T(512)S(1)} %get-tuple-element.316, s32[512]{0:T(512)S(1)} %get-tuple-element.317, ...), kind=kOutput, calls=%fused_computation.50.clone.1 | convolution fusion | flops 20148480 | bytes 52225 | tf_op jit(solution)/shard_map/while/body/eval_jaxpr/dot_general | solution.py:124
  65.4 1.9 %collective-permute-start = (f32[5,128]{1,0:T(8,128)S(1)}, f32[5,128]{1,0:T(8,128)S(1)}, u32[]{:S(2)}, u32[]{:S(2)}) collective-permute-start(f32[5,128]{1,0:T(8,128)S(1)} %slice.212), channel_id=1, source_target_pairs={{496,0},{0,16},{16,32},{32,48},{48,64},{64,80},{80,96},{96,112},{1... | collective-permute-start | bytes 7688 | tf_op jit(solution)/shard_map/ppermute | solution.py:10
  67.4 5.7 %collective-permute-done = f32[5,128]{1,0:T(8,128)S(1)} collective-permute-done((f32[5,128]{1,0:T(8,128)S(1)}, f32[5,128]{1,0:T(8,128)S(1)}, u32[]{:S(2)}, u32[]{:S(2)}) %collective-permute-start) | collective-permute-done | bytes 2592 | tf_op jit(solution)/shard_map/ppermute | solution.py:10
  73.1 6.9 %collective-permute-start.1 = (f32[4,128]{1,0:T(4,128)S(1)}, f32[4,128]{1,0:T(4,128)S(1)}, u32[]{:S(2)}, u32[]{:S(2)}) collective-permute-start(f32[4,128]{1,0:T(4,128)S(1)} %bitcast.161), channel_id=1, source_target_pairs={{15,0},{0,1},{1,2},{2,3},{3,4},{4,5},{5,6},{6,7},{7,8},{8,9},{9,10... | collective-permute-start | bytes 6152 | tf_op jit(solution)/shard_map/ppermute | solution.py:10
  82.9 3.5 %collective-permute-done.2 = f32[4,128]{1,0:T(4,128)S(1)} collective-permute-done((f32[4,128]{1,0:T(4,128)S(1)}, f32[4,128]{1,0:T(4,128)S(1)}, u32[]{:S(2)}, u32[]{:S(2)}) %collective-permute-start.2) | collective-permute-done | bytes 2080 | tf_op jit(solution)/shard_map/ppermute | solution.py:10
  86.4 1.9 %collective-permute-start.3 = (f32[5,128]{1,0:T(8,128)S(1)}, f32[5,128]{1,0:T(8,128)S(1)}, u32[]{:S(2)}, u32[]{:S(2)}) collective-permute-start(f32[5,128]{1,0:T(8,128)S(1)} %fusion.55), channel_id=1, source_target_pairs={{16,0},{32,16},{48,32},{64,48},{80,64},{96,80},{112,96},{128,112},... | collective-permute-start | bytes 7688 | tf_op jit(solution)/shard_map/ppermute | solution.py:10
  88.4 2.3 %collective-permute-done.3 = f32[5,128]{1,0:T(8,128)S(1)} collective-permute-done((f32[5,128]{1,0:T(8,128)S(1)}, f32[5,128]{1,0:T(8,128)S(1)}, u32[]{:S(2)}, u32[]{:S(2)}) %collective-permute-start.3) | collective-permute-done | bytes 2592 | tf_op jit(solution)/shard_map/ppermute | solution.py:10
  90.7 18.9 %while.27 = (s32[]{:T(128)}, f32[16,3,4,128]{3,2,1,0:T(4,128)S(1)}, f32[16,4,7,128]{3,2,1,0:T(8,128)S(1)}, f32[25,128]{1,0:T(8,128)S(1)}, s32[]{:T(128)}) while((s32[]{:T(128)}, f32[16,3,4,128]{3,2,1,0:T(4,128)S(1)}, f32[16,4,7,128]{3,2,1,0:T(8,128)S(1)}, f32[25,128]{1,0:T(8,128)S(1)}, s32[]{:T(128)}) %tuple.122), condition=%wide.region_10.11_spmd, body=%wide.region_6.10_spmd.sunk | while | flops 60314112 | bytes 2044485 | solution.py:167
  109.6 2.6 %slice_multiply_fusion.3 = f32[64,1,128]{2,0,1:T(8,128)S(1)} fusion(f32[64,3,128]{2,0,1:T(8,128)S(1)} %bitcast.121, f32[64,6,128]{2,0,1:T(8,128)S(1)} %bitcast.120, f32[]{:T(128)} %bitcast.34, f32[]{:T(128)} %bitcast.35, f32[]{:T(128)} %bitcast.37, f32[]{:T(128)} %bitcast.36), kind=kLoop, calls=%fused_computation.108 | loop fusion | flops 90112 | bytes 98320 | tf_op jit(solution)/shard_map/mul | solution.py:171
  113.0 5.0 %all-to-all-start.2 = ((f32[32,2,4,128]{3,1,2,0:T(2,128)}), f32[32,2,4,128]{3,1,2,0:T(2,128)S(1)}, u32[]{:S(2)}, u32[]{:S(2)}) async-start(f32[32,2,4,128]{3,1,2,0:T(2,128)} %copy.65), calls=%async_computation.2 | async-start | bytes 262144 | tf_op jit(solution)/shard_map/all_to_all | solution.py:175
  118.0 9.3 %all-to-all-done.2 = f32[32,2,4,128]{3,1,2,0:T(2,128)S(1)} async-done(((f32[32,2,4,128]{3,1,2,0:T(2,128)}), f32[32,2,4,128]{3,1,2,0:T(2,128)S(1)}, u32[]{:S(2)}, u32[]{:S(2)}) %all-to-all-start.2) | async-done | bytes 131104 | tf_op jit(solution)/shard_map/all_to_all | solution.py:175
  (321 shorter events, 30.4 us)
Async XLA Ops:
  0.6 0.7 copy-start.7
  1.3 15.3 %copy-start.1 = (s32[3,4096]{1,0:T(4,128)S(1)}, s32[3,4096]{1,0:T(4,128)}, u32[]{:S(2)}) copy-start(s32[3,4096]{1,0:T(4,128)} %param.17) | copy-start | bytes 147460
  1.6 0.7 copy-start.6
  3.7 21.4 %all-to-all-start.1 = ((s32[32,1,2]{2,1,0:T(1,128)}), s32[32,1,2]{2,1,0:T(1,128)S(1)}, u32[]{:S(2)}, u32[]{:S(2)}) async-start(s32[32,1,2]{2,1,0:T(1,128)} %bitcast.21), calls=%async_computation.1 | async-start | bytes 32768 | tf_op jit(solution)/shard_map/all_to_all | solution.py:105
  16.6 0.7 copy-start.2
  16.6 0.8 copy-start
  25.1 13.8 %all-to-all-start = ((f32[32,2,6,128]{3,1,2,0:T(2,128)}), f32[32,2,6,128]{3,1,2,0:T(2,128)S(1)}, u32[]{:S(2)}, u32[]{:S(2)}) async-start(f32[32,2,6,128]{3,1,2,0:T(2,128)} %copy.52), calls=%async_computation | async-start | bytes 393216 | tf_op jit(solution)/shard_map/all_to_all | solution.py:104
  65.4 7.7 %collective-permute-start = (f32[5,128]{1,0:T(8,128)S(1)}, f32[5,128]{1,0:T(8,128)S(1)}, u32[]{:S(2)}, u32[]{:S(2)}) collective-permute-start(f32[5,128]{1,0:T(8,128)S(1)} %slice.212), channel_id=1, source_target_pairs={{496,0},{0,16},{16,32},{32,48},{48,64},{64,80},{80,96},{96,112},{1... | collective-permute-start | bytes 7688 | tf_op jit(solution)/shard_map/ppermute | solution.py:10
  73.1 7.6 %collective-permute-start.1 = (f32[4,128]{1,0:T(4,128)S(1)}, f32[4,128]{1,0:T(4,128)S(1)}, u32[]{:S(2)}, u32[]{:S(2)}) collective-permute-start(f32[4,128]{1,0:T(4,128)S(1)} %bitcast.161), channel_id=1, source_target_pairs={{15,0},{0,1},{1,2},{2,3},{3,4},{4,5},{5,6},{6,7},{7,8},{8,9},{9,10... | collective-permute-start | bytes 6152 | tf_op jit(solution)/shard_map/ppermute | solution.py:10
  80.8 0.7 copy-start.5
  80.8 0.7 copy-start.4
  80.8 0.7 copy-start.8
  81.6 0.7 copy-start.3
  81.6 4.8 %collective-permute-start.2 = (f32[4,128]{1,0:T(4,128)S(1)}, f32[4,128]{1,0:T(4,128)S(1)}, u32[]{:S(2)}, u32[]{:S(2)}) collective-permute-start(f32[4,128]{1,0:T(4,128)S(1)} %bitcast.160), channel_id=1, source_target_pairs={{1,0},{2,1},{3,2},{4,3},{5,4},{6,5},{7,6},{8,7},{9,8},{10,9},{11,1... | collective-permute-start | bytes 6152 | tf_op jit(solution)/shard_map/ppermute | solution.py:10
  86.4 4.3 %collective-permute-start.3 = (f32[5,128]{1,0:T(8,128)S(1)}, f32[5,128]{1,0:T(8,128)S(1)}, u32[]{:S(2)}, u32[]{:S(2)}) collective-permute-start(f32[5,128]{1,0:T(8,128)S(1)} %fusion.55), channel_id=1, source_target_pairs={{16,0},{32,16},{48,32},{64,48},{80,64},{96,80},{112,96},{128,112},... | collective-permute-start | bytes 7688 | tf_op jit(solution)/shard_map/ppermute | solution.py:10
  113.0 14.4 %all-to-all-start.2 = ((f32[32,2,4,128]{3,1,2,0:T(2,128)}), f32[32,2,4,128]{3,1,2,0:T(2,128)S(1)}, u32[]{:S(2)}, u32[]{:S(2)}) async-start(f32[32,2,4,128]{3,1,2,0:T(2,128)} %copy.65), calls=%async_computation.2 | async-start | bytes 262144 | tf_op jit(solution)/shard_map/all_to_all | solution.py:175
where the time goes:
time: 130 us; the launch traced here: 129 us
  matrix products  37.5 us (29%)
  waiting for transfers between devices  35.3 us (27%)
  starting transfers between devices  32.6 us (25%)
  other arithmetic  10.5 us (8%)
  local copies, waits for them, and re-layouts  10.2 us (8%)
  loops' own time  2.34 us (2%)
    dot_general x16, matrix products, deposit(): lax.dot_general(plane_val * live_here[:, None], deep_val, (((0,), (0,)),...  24.5 us
    dot_general x16, matrix products, pull(): jnp.dot(stacked, field_plane, precision=lax.Precision.HIGHEST, preferred_...  13 us
    all_to_all x1, starting transfers between devices, on_device(): lax.all_to_all(out_counts, 'los', split_axis=0, concat_axis=0, tiled=True)  12.9 us
    ppermute x4, waiting for transfers between devices, passed_along(): return lax.ppermute(block, axis, route)  12.2 us
    ppermute x4, starting transfers between devices, passed_along(): return lax.ppermute(block, axis, route)  10.8 us
    all_to_all x1, waiting for transfers between devices, on_device(): lax.all_to_all(returned, 'los', split_axis=0, concat_axis=0, tiled=True)  9.3 us
    all_to_all x1, waiting for transfers between devices, on_device(): lax.all_to_all(outgoing, 'los', split_axis=0, concat_axis=0, tiled=True)  8.48 us
    all_to_all x1, waiting for transfers between devices, on_device(): lax.all_to_all(out_counts, 'los', split_axis=0, concat_axis=0, tiled=True)  5.3 us
  transfers between devices with their start and end apart: 7, of which 7 were waited for; matrix products, arithmetic and copies ran while one was open for 4% of the time, Pallas kernels for 0%

commit v1 on v0

v1 whole, which is shorter than its diff:
```python
import functools

import jax
import jax.numpy as jnp
from jax import lax
from jax.experimental import pallas as pl
from jax.experimental.pallas import tpu as pltpu
from jax.sharding import PartitionSpec as P

MESH = pl.DeviceIdType.MESH
F32 = jnp.float32
BF16 = jnp.bfloat16
LANES = 128
X = 4


def row_iota():
    return lax.broadcasted_iota(jnp.int32, (8, LANES), 0)


def split(values):
    high = values.astype(BF16)
    low = (values - high.astype(F32)).astype(BF16)
    return jnp.concatenate([high, low], axis=0)


def to_slots(dest, counts, cell, frac, off, slots, place, seen):
    sky_base = lax.axis_index("sky") * 4
    row = row_iota()
    empty = jnp.where(row == 0, -8.0, 0.0)
    for i in range(slots.shape[0]):
        slots[i] = empty
    for i in range(seen.shape[0]):
        seen[i] = 0
    lane = lax.broadcasted_iota(jnp.int32, (1, LANES), 1)
    for b in range(dest.shape[0]):
        lanes = slice(b * LANES, (b + 1) * LANES)
        los = jnp.where(lane < counts[b], (cell[0:1, lanes] + off[b : b + 1, :]) & 3, -8)
        slab = dest[b]
        rank = seen[slab]
        seen[slab] = rank + 1
        slot = slab * 2 + rank
        place[b] = slot
        cells = jnp.concatenate([los, cell[1:2, lanes] - sky_base, cell[2:3, lanes]], axis=0)
        slots[slot, 0:3] = cells.astype(F32)
        slots[slot, 3:6] = frac[:, lanes]


def from_slots(place, pulled, out_pos, out_vel):
    for b in range(place.shape[0]):
        values = pulled[place[b]]
        out_pos[:, b * LANES : (b + 1) * LANES] = values[:3]
        out_vel[b : b + 1, :] = values[3:]


def slot_rows(slots, i):
    return [slots[i, r : r + 1] for r in range(6)]


def one_hot_deep(deep):
    iota = lax.broadcasted_iota(jnp.int32, (LANES, LANES), 0).astype(F32)
    return jnp.where(iota == deep, 1.0, 0.0).astype(BF16)


def kernel(
    bias,
    rsd,
    slots,
    selection,
    galaxies,
    pulled,
    hot,
    grid,
    grid_side,
    rx,
    rx_side,
    total,
    rz,
    field,
    field_side,
    rates,
    send_x,
    recv_x,
    send_side,
    recv_side,
    send_z,
    recv_z,
    send_cz,
    recv_cz,
    send_f,
    recv_f,
    send_fs,
    recv_fs,
    send_rz,
    recv_rz,
    send_rx,
    recv_rx,
):
    z_size = grid.shape[1]
    sky_size = lax.axis_size("sky")
    los_here = lax.axis_index("los")
    sky_here = lax.axis_index("sky")
    z_here = los_here // X
    x_here = los_here % X
    sky_up = (sky_here + 1) % sky_size
    sky_down = (sky_here + sky_size - 1) % sky_size

    def x_peer(k):
        return z_here * X + (x_here + k) % X

    def z_peer(k):
        return ((z_here + k) % z_size) * X + x_here

    barrier = pltpu.get_barrier_semaphore()
    for k in range(X):
        if k:
            pl.semaphore_signal(
                barrier, inc=1, device_id=(x_peer(k), sky_here), device_id_type=MESH
            )
        for sky_to in (sky_up, sky_down):
            pl.semaphore_signal(barrier, inc=1, device_id=(x_peer(k), sky_to), device_id_type=MESH)
    for k in range(1, z_size):
        pl.semaphore_signal(barrier, inc=1, device_id=(z_peer(k), sky_here), device_id_type=MESH)

    row4 = lax.broadcasted_iota(jnp.int32, (4, LANES), 0)

    def by_row(scalars):
        value = jnp.full((4, LANES), scalars[3], F32)
        for i in (0, 1, 2):
            value = jnp.where(row4 == i, scalars[i], value)
        return value

    rates[x_here, z_here] = by_row(rsd)
    row = row_iota().astype(F32)

    def paint(t, previous):
        tables, hots = [], []
        for slot in (0, 1):
            los, sky, deep, f_los, f_sky, f_deep = slot_rows(slots, t * 2 + slot)
            h_los = jnp.where(row == los, 1.0 - f_los, 0.0) + jnp.where(row == los + 1, f_los, 0.0)
            h_sky = jnp.where(row == sky, 1.0 - f_sky, 0.0) + jnp.where(row == sky + 1, f_sky, 0.0)
            lower, upper = h_los * (1.0 - f_deep), h_los * f_deep
            parts = []
            for s in range(5):
                parts += [h_sky[s : s + 1] * lower, h_sky[s : s + 1] * upper]
            tables.append(split(jnp.concatenate(parts, axis=0)))
            one_hot = one_hot_deep(deep)
            hot[t, :, slot * LANES : (slot + 1) * LANES] = one_hot
            hots.append(one_hot)
        result = lax.dot_general(
            jnp.concatenate(tables, axis=1),
            jnp.concatenate(hots, axis=1),
            (((1,), (1,)), ((), ())),
            preferred_element_type=F32,
        )
        result = result[:80] + result[80:]
        planes = []
        for s in range(5):
            lower, upper = result[s * 16 : s * 16 + 8], result[s * 16 + 8 : s * 16 + 16]
            planes.append(lower + pltpu.roll(upper, 1, 1))
        return planes

    def paint_step(step, previous):
        for i in range(2):
            z = step * 2 + i
            for x in range(X):
                planes = paint(z * X + x, previous)
                for s in range(5):
                    carried = jnp.where(row == 0, pltpu.roll(previous[s], 4, 0), 0.0)
                    whole = (planes[s] + carried)[:4]
                    if s < 4:
                        grid[x, z, s] = whole
                    else:
                        grid_side[x, z] = whole
                previous = planes
        return tuple(previous)

    zero = jnp.zeros((8, LANES), F32)
    last = lax.fori_loop(0, z_size // 2, paint_step, (zero,) * 5)
    for s in range(5):
        carried = jnp.where(row == 0, pltpu.roll(last[s], 4, 0), 0.0)[:4]
        if s < 4:
            grid[0, 0, s] = grid[0, 0, s] + carried
        else:
            grid_side[0, 0] = grid_side[0, 0] + carried

    pl.semaphore_wait(barrier, 3 + 2 * X + z_size - 1)

    def remote(src, dst, send_sem, recv_sem, los_to, sky_to):
        return pltpu.make_async_remote_copy(
            src_ref=src,
            dst_ref=dst,
            send_sem=send_sem,
            recv_sem=recv_sem,
            device_id=(los_to, sky_to),
            device_id_type=MESH,
        )

    x_copies, side_copies = {}, {}
    for k in (2, 1, 3, 0):
        x_to = (x_here + k) % X
        if k:
            x_copies[k] = remote(
                grid.at[x_to], rx.at[k - 1], send_x.at[k - 1], recv_x.at[k - 1], x_peer(k), sky_here
            )
            x_copies[k].start()
        side_copies[k] = remote(
            grid_side.at[x_to],
            rx_side.at[k],
            send_side.at[k],
            recv_side.at[k],
            x_peer(k),
            sky_up,
        )
        side_copies[k].start()
    rate_z = {}
    for k in range(1, z_size):
        rate_z[k] = remote(
            rates.at[x_here, z_here],
            rates.at[x_here, z_here],
            send_rz.at[k - 1],
            recv_rz.at[k - 1],
            z_peer(k),
            sky_here,
        )
        rate_z[k].start()
    for k in range(X):
        if k:
            x_copies[k].wait_recv()
        side_copies[k].wait_recv()

    def gather_x(z):
        for s in range(4):
            value = grid[x_here, z, s]
            for k in range(1, X):
                value = value + rx[k - 1, z, s]
            if s == 0:
                for k in range(X):
                    value = value + rx_side[k, z]
            total[z, s] = value

    order = sorted(range(1, z_size), key=lambda k: -min(k, z_size - k))
    z_copies = {}
    for k in order:
        z_to = (z_here + k) % z_size
        gather_x(z_to)
        z_copies[k] = remote(
            total.at[z_to], rz.at[k - 1], send_z.at[k - 1], recv_z.at[k - 1], z_peer(k), sky_here
        )
        z_copies[k].start()
    gather_x(z_here)

    for k in range(1, z_size):
        rate_z[k].wait_recv()
    rate_x = {}
    for k in range(1, X):
        rate_x[k] = remote(
            rates.at[x_here],
            rates.at[x_here],
            send_rx.at[k - 1],
            recv_rx.at[k - 1],
            x_peer(k),
            sky_here,
        )
        rate_x[k].start()

    exponent = by_row(bias)
    for k in range(1, z_size):
        z_copies[k].wait_recv()
    for s in range(4):
        density = total[z_here, s]
        for k in range(1, z_size):
            density = density + rz[k - 1, s]
        mean = jnp.concatenate([selection[l, s : s + 1] for l in range(4)], axis=0)
        seen = jnp.concatenate([galaxies[l, s : s + 1] for l in range(4)], axis=0).astype(F32)
        shifted = density + 0.5
        intensity = mean * jnp.exp(exponent * jnp.log(shifted))
        field[x_here, z_here, s] = (1.0 - seen / intensity) * exponent * intensity / shifted

    cz_copies = {}
    for k in order:
        cz_copies[k] = remote(
            field.at[x_here, z_here],
            field.at[x_here, z_here],
            send_cz.at[k - 1],
            recv_cz.at[k - 1],
            z_peer(k),
            sky_here,
        )
        cz_copies[k].start()
    f_copies, fs_copies = {}, {}
    for j in sorted(range(z_size), key=lambda k: min(k, z_size - k)):
        if j:
            cz_copies[j].wait_recv()
        z_from = (z_here + z_size - j) % z_size
        for k in (2, 1, 3, 0):
            if k:
                f_copies[j, k] = remote(
                    field.at[x_here, z_from],
                    field.at[x_here, z_from],
                    send_f.at[j, k - 1],
                    recv_f.at[j, k - 1],
                    x_peer(k),
                    sky_here,
                )
                f_copies[j, k].start()
            fs_copies[j, k] = remote(
                field.at[x_here, z_from, 0],
                field_side.at[x_here, z_from],
                send_fs.at[j, k],
                recv_fs.at[j, k],
                x_peer(k),
                sky_down,
            )
            fs_copies[j, k].start()
    for k in range(1, X):
        rate_x[k].wait_recv()
    for j, k in f_copies:
        f_copies[j, k].wait_recv()
    for j, k in fs_copies:
        fs_copies[j, k].wait_recv()

    def pull(z, x):
        t = z * X + x
        z_next, x_next = (z, x + 1) if x + 1 < X else (lax.rem(z + 1, z_size), 0)
        rows = []
        for s in range(5):
            if s < 4:
                value = jnp.concatenate([field[x, z, s], field[x_next, z_next, s]], axis=0)
            else:
                value = jnp.concatenate([field_side[x, z], field_side[x_next, z_next]], axis=0)
            rows += [value, pltpu.roll(value, LANES - 1, 1)]
        picked = jnp.dot(
            split(jnp.concatenate(rows, axis=0)), hot[t], preferred_element_type=F32
        )
        picked = picked[:80] + picked[80:]
        rate = jnp.concatenate([rates[x, z], jnp.zeros((4, LANES), F32)], axis=0)
        for slot in (0, 1):
            los, sky, deep, f_los, f_sky, f_deep = slot_rows(slots, t * 2 + slot)
            at, above = row == los, row == los + 1
            h_los = jnp.where(at, 1.0 - f_los, 0.0) + jnp.where(above, f_los, 0.0)
            d_los = jnp.where(above, 1.0, 0.0) - jnp.where(at, 1.0, 0.0)
            r_los = jnp.where(at, rate, 0.0)
            at, above = row == sky, row == sky + 1
            h_sky = jnp.where(at, 1.0 - f_sky, 0.0) + jnp.where(above, f_sky, 0.0)
            d_sky = jnp.where(above, 1.0, 0.0) - jnp.where(at, 1.0, 0.0)
            lanes = slice(slot * LANES, (slot + 1) * LANES)
            val, val_sky, val_deep = zero, zero, zero
            for s in range(5):
                here = picked[s * 16 : s * 16 + 8, lanes]
                step = picked[s * 16 + 8 : s * 16 + 16, lanes] - here
                mixed = here + f_deep * step
                val = val + h_sky[s : s + 1] * mixed
                val_sky = val_sky + d_sky[s : s + 1] * mixed
                val_deep = val_deep + h_sky[s : s + 1] * step
            g_los = jnp.sum(d_los * val, axis=0, keepdims=True)
            g_sky = jnp.sum(h_los * val_sky, axis=0, keepdims=True)
            g_deep = jnp.sum(h_los * val_deep, axis=0, keepdims=True)
            speed = jnp.sum(r_los, axis=0, keepdims=True) * g_los
            pulled[t * 2 + slot] = jnp.concatenate([g_los, g_sky, g_deep, speed], axis=0)

    def pull_step(step, unused):
        for i in range(2):
            for x in range(X):
                pull(step * 2 + i, x)
        return unused

    lax.fori_loop(0, z_size // 2, pull_step, 0)

    for copies in (
        x_copies,
        side_copies,
        rate_z,
        z_copies,
        rate_x,
        cz_copies,
        f_copies,
        fs_copies,
    ):
        for copy in copies.values():
            copy.wait_send()


def on_device(
    part_cell,
    part_frac,
    los_offset,
    block_dest,
    block_count,
    selection,
    galaxy_counts,
    bias_exp,
    rsd_factor,
):
    los_size = lax.axis_size("los")
    z_size = los_size // X
    blocks = block_dest.shape[0]
    vmem = pl.BlockSpec(memory_space=pltpu.VMEM)
    smem = pl.BlockSpec(memory_space=pltpu.SMEM)
    dma = pltpu.SemaphoreType.DMA
    slots, place = pl.pallas_call(
        to_slots,
        out_shape=(
            jax.ShapeDtypeStruct((2 * los_size, 8, LANES), F32),
            jax.ShapeDtypeStruct((blocks,), jnp.int32),
        ),
        in_specs=[smem] * 2 + [vmem] * 3,
        out_specs=(vmem, smem),
        scratch_shapes=[pltpu.SMEM((los_size,), jnp.int32)],
        name="to_slots",
    )(block_dest, block_count, part_cell, part_frac, los_offset.reshape(blocks, LANES))
    pulled = pl.pallas_call(
        kernel,
        out_shape=jax.ShapeDtypeStruct((2 * los_size, 4, LANES), F32),
        in_specs=[smem] * 2 + [vmem] * 3,
        out_specs=vmem,
        scratch_shapes=[
            pltpu.VMEM((los_size, LANES, 2 * LANES), BF16),
            pltpu.VMEM((X, z_size, 4, 4, LANES), F32),
            pltpu.VMEM((X, z_size, 4, LANES), F32),
            pltpu.VMEM((X - 1, z_size, 4, 4, LANES), F32),
            pltpu.VMEM((X, z_size, 4, LANES), F32),
            pltpu.VMEM((z_size, 4, 4, LANES), F32),
            pltpu.VMEM((z_size - 1, 4, 4, LANES), F32),
            pltpu.VMEM((X, z_size, 4, 4, LANES), F32),
            pltpu.VMEM((X, z_size, 4, LANES), F32),
            pltpu.VMEM((X, z_size, 4, LANES), F32),
            dma((X - 1,)),
            dma((X - 1,)),
            dma((X,)),
            dma((X,)),
            dma((z_size - 1,)),
            dma((z_size - 1,)),
            dma((z_size - 1,)),
            dma((z_size - 1,)),
            dma((z_size, X - 1)),
            dma((z_size, X - 1)),
            dma((z_size, X)),
            dma((z_size, X)),
            dma((z_size - 1,)),
            dma((z_size - 1,)),
            dma((X - 1,)),
            dma((X - 1,)),
        ],
        compiler_params=pltpu.CompilerParams(collective_id=0, has_side_effects=True),
        name="adjoint",
    )(bias_exp, rsd_factor, slots, selection, galaxy_counts)
    grad_pos, grad_vel = pl.pallas_call(
        from_slots,
        out_shape=(
            jax.ShapeDtypeStruct(part_frac.shape, F32),
            jax.ShapeDtypeStruct((blocks, LANES), F32),
        ),
        in_specs=[smem, vmem],
        out_specs=(vmem, vmem),
        name="from_slots",
    )(place, pulled)
    return grad_pos, grad_vel.reshape(-1)


def solution(mesh):
    return jax.shard_map(
        on_device,
        mesh=mesh,
        in_specs=(
            P(None, ("los", "sky")),
            P(None, ("los", "sky")),
            P(("los", "sky")),
            P(("los", "sky")),
            P(("los", "sky")),
            P("los", "sky", None),
            P("los", "sky", None),
            P("los"),
            P("los"),
        ),
        out_specs=(P(None, ("los", "sky")), P(("los", "sky"))),
        check_vma=False,
    )
```

time: 130 us -> 41.5 us (0.32)
  Pallas kernels: 0 us -> 40.6 us
  matrix products: 37.5 us -> 0 us
  waiting for transfers between devices: 35.3 us -> 0 us
  starting transfers between devices: 32.6 us -> 0 us
  other arithmetic: 10.5 us -> 0 us
  local copies, waits for them, and re-layouts: 10.2 us -> 0 us
  loops' own time: 2.34 us -> 0 us
    pallas_call x0 -> x3, Pallas kernels: none -> 40.6 us  [the longest x1 37.3 us: on_device(): pl.pallas_call(kernel, out_shape=jax.ShapeDtypeStruct((2 * los_size, 4, L...]
    dot_general x32 -> x0, matrix products: 37.5 us -> none  [the longest x16 24.5 us: deposit(): lax.dot_general(plane_val * live_here[:, None], deep_val, (((0,), (0,)),...]
    all_to_all x3 -> x0, waiting for transfers between devices: 23.1 us -> none  [the longest x1 9.3 us: on_device(): lax.all_to_all(returned, 'los', split_axis=0, concat_axis=0, tiled=True)]
    all_to_all x3 -> x0, starting transfers between devices: 21.8 us -> none  [the longest x1 12.9 us: on_device(): lax.all_to_all(out_counts, 'los', split_axis=0, concat_axis=0, tiled=True)]
    ppermute x4 -> x0, waiting for transfers between devices: 12.2 us -> none  [passed_along(): return lax.ppermute(block, axis, route)]
    ppermute x4 -> x0, starting transfers between devices: 10.8 us -> none  [passed_along(): return lax.ppermute(block, axis, route)]
    mul x36 -> x0, other arithmetic: 4.19 us -> none  [the longest x1 2.55 us: on_device(): rate_each * pulled[:, 0]]
    unnamed x18 -> x0, local copies, waits for them, and re-layouts: 3.36 us -> none
  transfers between devices with their start and end apart: 7 -> 0, of which waited for: 7 -> 0; matrix products, arithmetic and copies ran while one was open for 4% -> 0% of each run, Pallas kernels for 0% -> 0%
where the time goes in v1:
time: 41.5 us; the launch traced here: 41.3 us
  Pallas kernels  40.6 us (98%)
  between operations  0.65 us (2%)
    pallas_call x1, Pallas kernels, on_device(): pl.pallas_call(kernel, out_shape=jax.ShapeDtypeStruct((2 * los_size, 4, L...  37.3 us
    pallas_call x1, Pallas kernels, on_device(): pl.pallas_call(to_slots, out_shape=(jax.ShapeDtypeStruct((2 * los_size, 8...  1.73 us
    pallas_call x1, Pallas kernels, on_device(): pl.pallas_call(from_slots, out_shape=(jax.ShapeDtypeStruct(part_frac.shap...  1.58 us

profile of v1, /device:TPU:25, one launch (start us, length us, event | category | flops | bytes accessed | tf_op | source)
XLA Modules:
  0.0 41.3 jit_solution(1377100699916388071)
XLA Ops:
  0.6 1.7 %to_slots.1 = (f32[64,8,128]{2,1,0:T(8,128)}, s32[32]{0:T(128)}) custom-call(s32[32]{0:T(128)} %dest.1, s32[32]{0:T(128)} %counts.1, s32[3,4096]{1,0:T(4,128)} %cell.1, f32[3,4096]{1,0:T(4,128)} %frac.1, s32[32,128]{1,0:T(8,128)} %bitcast.2), custom_call_target="tpu_custom_call" | custom-call | tf_op jit(solution)/shard_map/to_slots/pallas_call | solution.py:401
  2.4 37.3 %adjoint.1.pulled = f32[64,4,128]{2,1,0:T(4,128)} custom-call(f32[4]{0:T(128)} %bias.1, f32[4]{0:T(128)} %rsd.1, f32[64,8,128]{2,1,0:T(8,128)} %get-tuple-element.7.slots, f32[4,4,128]{2,1,0:T(4,128)} %selection.1, s32[4,4,128]{2,1,0:T(4,128)} %galaxies.1), custom_call_target="tpu_custom_call" | custom-call | tf_op jit(solution)/shard_map/adjoint/pallas_call | solution.py:412
  39.7 1.6 %from_slots.1 = (f32[3,4096]{1,0:T(4,128)}, f32[32,128]{1,0:T(8,128)}) custom-call(s32[32]{0:T(128)} %get-tuple-element.6.place, f32[64,4,128]{2,1,0:T(4,128)} %adjoint.1.pulled), custom_call_target="tpu_custom_call" | custom-call | tf_op jit(solution)/shard_map/from_slots/pallas_call | solution.py:448

commit v2 on v1

--- a/solution.py
+++ b/solution.py
@@ -1,5 +1,3 @@
-import functools
-
 import jax
 import jax.numpy as jnp
 from jax import lax
@@ -24,7 +22,21 @@
     return jnp.concatenate([high, low], axis=0)
 
 
-def to_slots(dest, counts, cell, frac, off, slots, place, seen):
+def fetch(sources, targets, sems):
+    copies = [
+        pltpu.make_async_copy(source, target, sems.at[i])
+        for i, (source, target) in enumerate(zip(sources, targets, strict=True))
+    ]
+    for copy in copies:
+        copy.start()
+    return copies
+
+
+def to_slots(dest_in, counts_in, cell_in, frac_in, off_in, slots, place, *scratch):
+    dest, counts, cell, frac, off, seen, sems = scratch
+    copies = fetch(
+        (dest_in, counts_in, cell_in, frac_in, off_in), (dest, counts, cell, frac, off), sems
+    )
     sky_base = lax.axis_index("sky") * 4
     row = row_iota()
     empty = jnp.where(row == 0, -8.0, 0.0)
@@ -32,6 +44,8 @@
         slots[i] = empty
     for i in range(seen.shape[0]):
         seen[i] = 0
+    for copy in copies:
+        copy.wait()
     lane = lax.broadcasted_iota(jnp.int32, (1, LANES), 1)
     for b in range(dest.shape[0]):
         lanes = slice(b * LANES, (b + 1) * LANES)
@@ -63,12 +77,17 @@
 
 
 def kernel(
+    bias_in,
+    rsd_in,
+    slots,
+    selection_in,
+    galaxies_in,
+    pulled,
     bias,
     rsd,
-    slots,
     selection,
     galaxies,
-    pulled,
+    fetch_sems,
     hot,
     grid,
     grid_side,
@@ -122,6 +141,9 @@
     for k in range(1, z_size):
         pl.semaphore_signal(barrier, inc=1, device_id=(z_peer(k), sky_here), device_id_type=MESH)
 
+    fetched = fetch(
+        (bias_in, rsd_in, selection_in, galaxies_in), (bias, rsd, selection, galaxies), fetch_sems
+    )
     row4 = lax.broadcasted_iota(jnp.int32, (4, LANES), 0)
 
     def by_row(scalars):
@@ -130,10 +152,9 @@
             value = jnp.where(row4 == i, scalars[i], value)
         return value
 
-    rates[x_here, z_here] = by_row(rsd)
     row = row_iota().astype(F32)
 
-    def paint(t, previous):
+    def paint(t):
         tables, hots = [], []
         for slot in (0, 1):
             los, sky, deep, f_los, f_sky, f_deep = slot_rows(slots, t * 2 + slot)
@@ -160,30 +181,31 @@
             planes.append(lower + pltpu.roll(upper, 1, 1))
         return planes
 
+    order = [(z_size // 2 - 1 + j) % z_size for j in range(z_size)]
+
     def paint_step(step, previous):
         for i in range(2):
-            z = step * 2 + i
+            j = step * 2 + i
+            z = lax.rem(z_here + order[0] + j, z_size)
             for x in range(X):
-                planes = paint(z * X + x, previous)
+                planes = paint(z * X + x)
                 for s in range(5):
                     carried = jnp.where(row == 0, pltpu.roll(previous[s], 4, 0), 0.0)
                     whole = (planes[s] + carried)[:4]
                     if s < 4:
-                        grid[x, z, s] = whole
+                        grid[x, j, s] = whole
                     else:
-                        grid_side[x, z] = whole
+                        grid_side[x, j] = whole
                 previous = planes
         return tuple(previous)
 
     zero = jnp.zeros((8, LANES), F32)
-    last = lax.fori_loop(0, z_size // 2, paint_step, (zero,) * 5)
-    for s in range(5):
-        carried = jnp.where(row == 0, pltpu.roll(last[s], 4, 0), 0.0)[:4]
-        if s < 4:
-            grid[0, 0, s] = grid[0, 0, s] + carried
-        else:
-            grid_side[0, 0] = grid_side[0, 0] + carried
-
+    before = lax.rem(z_here + order[-1], z_size)
+    lax.fori_loop(0, z_size // 2, paint_step, tuple(paint(before * X + X - 1)))
+
+    for copy in fetched:
+        copy.wait()
+    rates[x_here, z_here] = by_row(rsd)
     pl.semaphore_wait(barrier, 3 + 2 * X + z_size - 1)
 
     def remote(src, dst, send_sem, recv_sem, los_to, sky_to):
@@ -196,24 +218,31 @@
             device_id_type=MESH,
         )
 
-    x_copies, side_copies = {}, {}
-    for k in (2, 1, 3, 0):
-        x_to = (x_here + k) % X
-        if k:
-            x_copies[k] = remote(
-                grid.at[x_to], rx.at[k - 1], send_x.at[k - 1], recv_x.at[k - 1], x_peer(k), sky_here
+    groups = [range(i, i + 2) for i in range(0, z_size, 2)]
+    x_copies, side_copies, z_copies, rate_z = {}, {}, {}, {}
+    for g, group in enumerate(groups):
+        part = pl.ds(group[0], len(group))
+        for k in (2, 1, 3, 0):
+            x_to = (x_here + k) % X
+            if k:
+                x_copies[g, k] = remote(
+                    grid.at[x_to, part],
+                    rx.at[k - 1, part],
+                    send_x.at[g, k - 1],
+                    recv_x.at[g, k - 1],
+                    x_peer(k),
+                    sky_here,
+                )
+                x_copies[g, k].start()
+            side_copies[g, k] = remote(
+                grid_side.at[x_to, part],
+                rx_side.at[k, part],
+                send_side.at[g, k],
+                recv_side.at[g, k],
+                x_peer(k),
+                sky_up,
             )
-            x_copies[k].start()
-        side_copies[k] = remote(
-            grid_side.at[x_to],
-            rx_side.at[k],
-            send_side.at[k],
-            recv_side.at[k],
-            x_peer(k),
-            sky_up,
-        )
-        side_copies[k].start()
-    rate_z = {}
+            side_copies[g, k].start()
     for k in range(1, z_size):
         rate_z[k] = remote(
             rates.at[x_here, z_here],
@@ -224,31 +253,32 @@
             sky_here,
         )
         rate_z[k].start()
-    for k in range(X):
-        if k:
-            x_copies[k].wait_recv()
-        side_copies[k].wait_recv()
-
-    def gather_x(z):
-        for s in range(4):
-            value = grid[x_here, z, s]
-            for k in range(1, X):
-                value = value + rx[k - 1, z, s]
-            if s == 0:
-                for k in range(X):
-                    value = value + rx_side[k, z]
-            total[z, s] = value
-
-    order = sorted(range(1, z_size), key=lambda k: -min(k, z_size - k))
-    z_copies = {}
-    for k in order:
-        z_to = (z_here + k) % z_size
-        gather_x(z_to)
-        z_copies[k] = remote(
-            total.at[z_to], rz.at[k - 1], send_z.at[k - 1], recv_z.at[k - 1], z_peer(k), sky_here
-        )
-        z_copies[k].start()
-    gather_x(z_here)
+
+    for g, group in enumerate(groups):
+        for k in range(X):
+            if k:
+                x_copies[g, k].wait_recv()
+            side_copies[g, k].wait_recv()
+        for j in group:
+            for s in range(4):
+                value = grid[x_here, j, s]
+                for k in range(1, X):
+                    value = value + rx[k - 1, j, s]
+                if s == 0:
+                    for k in range(X):
+                        value = value + rx_side[k, j]
+                total[j, s] = value
+            k = order[j]
+            if k:
+                z_copies[k] = remote(
+                    total.at[j],
+                    rz.at[k - 1],
+                    send_z.at[k - 1],
+                    recv_z.at[k - 1],
+                    z_peer(k),
+                    sky_here,
+                )
+                z_copies[k].start()
 
     for k in range(1, z_size):
         rate_z[k].wait_recv()
@@ -268,7 +298,7 @@
     for k in range(1, z_size):
         z_copies[k].wait_recv()
     for s in range(4):
-        density = total[z_here, s]
+        density = total[order.index(0), s]
         for k in range(1, z_size):
             density = density + rz[k - 1, s]
         mean = jnp.concatenate([selection[l, s : s + 1] for l in range(4)], axis=0)
@@ -278,7 +308,7 @@
         field[x_here, z_here, s] = (1.0 - seen / intensity) * exponent * intensity / shifted
 
     cz_copies = {}
-    for k in order:
+    for k in sorted(range(1, z_size), key=lambda k: -min(k, z_size - k)):
         cz_copies[k] = remote(
             field.at[x_here, z_here],
             field.at[x_here, z_here],
@@ -315,14 +345,9 @@
             fs_copies[j, k].start()
     for k in range(1, X):
         rate_x[k].wait_recv()
-    for j, k in f_copies:
-        f_copies[j, k].wait_recv()
-    for j, k in fs_copies:
-        fs_copies[j, k].wait_recv()
-
     def pull(z, x):
         t = z * X + x
-        z_next, x_next = (z, x + 1) if x + 1 < X else (lax.rem(z + 1, z_size), 0)
+        z_next, x_next = (z, x + 1) if x + 1 < X else ((z + 1) % z_size, 0)
         rows = []
         for s in range(5):
             if s < 4:
@@ -359,13 +384,18 @@
             speed = jnp.sum(r_los, axis=0, keepdims=True) * g_los
             pulled[t * 2 + slot] = jnp.concatenate([g_los, g_sky, g_deep, speed], axis=0)
 
-    def pull_step(step, unused):
-        for i in range(2):
+    waited = set()
+    for g in range(z_size // 2):
+        for j in (0, g + 1, z_size - g - 1):
+            if j not in waited:
+                waited.add(j)
+                for k in range(X):
+                    if k:
+                        f_copies[j, k].wait_recv()
+                    fs_copies[j, k].wait_recv()
+        for z in ((z_here + z_size - g - 1) % z_size, (z_here + g) % z_size):
             for x in range(X):
-                pull(step * 2 + i, x)
-        return unused
-
-    lax.fori_loop(0, z_size // 2, pull_step, 0)
+                pull(z, x)
 
     for copies in (
         x_copies,
@@ -397,6 +427,7 @@
     blocks = block_dest.shape[0]
     vmem = pl.BlockSpec(memory_space=pltpu.VMEM)
     smem = pl.BlockSpec(memory_space=pltpu.SMEM)
+    hbm = pl.BlockSpec(memory_space=pltpu.HBM)
     dma = pltpu.SemaphoreType.DMA
     slots, place = pl.pallas_call(
         to_slots,
@@ -404,17 +435,30 @@
             jax.ShapeDtypeStruct((2 * los_size, 8, LANES), F32),
             jax.ShapeDtypeStruct((blocks,), jnp.int32),
         ),
-        in_specs=[smem] * 2 + [vmem] * 3,
+        in_specs=[hbm] * 5,
         out_specs=(vmem, smem),
-        scratch_shapes=[pltpu.SMEM((los_size,), jnp.int32)],
+        scratch_shapes=[
+            pltpu.SMEM((blocks,), jnp.int32),
+            pltpu.SMEM((blocks,), jnp.int32),
+            pltpu.VMEM(part_cell.shape, jnp.int32),
+            pltpu.VMEM(part_frac.shape, F32),
+            pltpu.VMEM((blocks, LANES), jnp.int32),
+            pltpu.SMEM((los_size,), jnp.int32),
+            dma((5,)),
+        ],
         name="to_slots",
     )(block_dest, block_count, part_cell, part_frac, los_offset.reshape(blocks, LANES))
     pulled = pl.pallas_call(
         kernel,
         out_shape=jax.ShapeDtypeStruct((2 * los_size, 4, LANES), F32),
-        in_specs=[smem] * 2 + [vmem] * 3,
+        in_specs=[hbm, hbm, vmem, hbm, hbm],
         out_specs=vmem,
         scratch_shapes=[
+            pltpu.SMEM(bias_exp.shape, F32),
+            pltpu.SMEM(rsd_factor.shape, F32),
+            pltpu.VMEM(selection.shape, F32),
+            pltpu.VMEM(galaxy_counts.shape, jnp.int32),
+            dma((4,)),
             pltpu.VMEM((los_size, LANES, 2 * LANES), BF16),
             pltpu.VMEM((X, z_size, 4, 4, LANES), F32),
             pltpu.VMEM((X, z_size, 4, LANES), F32),
@@ -425,10 +469,10 @@
             pltpu.VMEM((X, z_size, 4, 4, LANES), F32),
             pltpu.VMEM((X, z_size, 4, LANES), F32),
             pltpu.VMEM((X, z_size, 4, LANES), F32),
-            dma((X - 1,)),
-            dma((X - 1,)),
-            dma((X,)),
-            dma((X,)),
+            dma((z_size // 2, X - 1)),
+            dma((z_size // 2, X - 1)),
+            dma((z_size // 2, X)),
+            dma((z_size // 2, X)),
             dma((z_size - 1,)),
             dma((z_size - 1,)),
             dma((z_size - 1,)),
@@ -442,7 +486,9 @@
             dma((X - 1,)),
             dma((X - 1,)),
         ],
-        compiler_params=pltpu.CompilerParams(collective_id=0, has_side_effects=True),
+        compiler_params=pltpu.CompilerParams(
+            collective_id=0, has_side_effects=True
+        ),
         name="adjoint",
     )(bias_exp, rsd_factor, slots, selection, galaxy_counts)
     grad_pos, grad_vel = pl.pallas_call(

time: 41.5 us -> 40.1 us (0.966)
  Pallas kernels: 40.6 us -> 39.2 us
    pallas_call x1, Pallas kernels: 37.3 us -> 35.9 us  [on_device(): pl.pallas_call(kernel, out_shape=jax.ShapeDtypeStruct((2 * los_size, 4, L...]
where the time goes in v2:
time: 40.1 us; the launch traced here: 39.9 us
  Pallas kernels  39.2 us (98%)
  between operations  0.65 us (2%)
    pallas_call x1, Pallas kernels, on_device(): pl.pallas_call(kernel, out_shape=jax.ShapeDtypeStruct((2 * los_size, 4, L...  35.9 us
    pallas_call x1, Pallas kernels, on_device(): pl.pallas_call(to_slots, out_shape=(jax.ShapeDtypeStruct((2 * los_size, 8...  1.76 us
    pallas_call x1, Pallas kernels, on_device(): pl.pallas_call(from_slots, out_shape=(jax.ShapeDtypeStruct(part_frac.shap...  1.58 us

profile of v2, /device:TPU:25, one launch (start us, length us, event | category | flops | bytes accessed | tf_op | source)
XLA Modules:
  0.0 39.9 jit_solution(10325641894111566978)
XLA Ops:
  0.6 1.8 %to_slots.1 = (f32[64,8,128]{2,1,0:T(8,128)}, s32[32]{0:T(128)}) custom-call(s32[32]{0:T(128)} %dest_in.1, s32[32]{0:T(128)} %counts_in.1, s32[3,4096]{1,0:T(4,128)} %cell_in.1, f32[3,4096]{1,0:T(4,128)} %frac_in.1, s32[32,128]{1,0:T(8,128)} %bitcast.2), custom_call_target="tpu_custom_call" | custom-call | tf_op jit(solution)/shard_map/to_slots/pallas_call | solution.py:432
  2.4 35.9 %adjoint.1.pulled = f32[64,4,128]{2,1,0:T(4,128)} custom-call(f32[4]{0:T(128)} %bias_in.1, f32[4]{0:T(128)} %rsd_in.1, f32[64,8,128]{2,1,0:T(8,128)} %get-tuple-element.7.slots, f32[4,4,128]{2,1,0:T(4,128)} %selection_in.1, s32[4,4,128]{2,1,0:T(4,128)} %galaxies_in.1), custom_call_target="tpu_custom_call" | custom-call | tf_op jit(solution)/shard_map/adjoint/pallas_call | solution.py:451
  38.3 1.6 %from_slots.1 = (f32[3,4096]{1,0:T(4,128)}, f32[32,128]{1,0:T(8,128)}) custom-call(s32[32]{0:T(128)} %get-tuple-element.6.place, f32[64,4,128]{2,1,0:T(4,128)} %adjoint.1.pulled), custom_call_target="tpu_custom_call" | custom-call | tf_op jit(solution)/shard_map/from_slots/pallas_call | solution.py:494

commit v3 on v2

--- a/solution.py
+++ b/solution.py
@@ -32,43 +32,31 @@
     return copies
 
 
-def to_slots(dest_in, counts_in, cell_in, frac_in, off_in, slots, place, *scratch):
-    dest, counts, cell, frac, off, seen, sems = scratch
-    copies = fetch(
-        (dest_in, counts_in, cell_in, frac_in, off_in), (dest, counts, cell, frac, off), sems
-    )
-    sky_base = lax.axis_index("sky") * 4
-    row = row_iota()
-    empty = jnp.where(row == 0, -8.0, 0.0)
-    for i in range(slots.shape[0]):
-        slots[i] = empty
-    for i in range(seen.shape[0]):
-        seen[i] = 0
-    for copy in copies:
-        copy.wait()
-    lane = lax.broadcasted_iota(jnp.int32, (1, LANES), 1)
-    for b in range(dest.shape[0]):
-        lanes = slice(b * LANES, (b + 1) * LANES)
-        los = jnp.where(lane < counts[b], (cell[0:1, lanes] + off[b : b + 1, :]) & 3, -8)
-        slab = dest[b]
-        rank = seen[slab]
-        seen[slab] = rank + 1
-        slot = slab * 2 + rank
-        place[b] = slot
-        cells = jnp.concatenate([los, cell[1:2, lanes] - sky_base, cell[2:3, lanes]], axis=0)
-        slots[slot, 0:3] = cells.astype(F32)
-        slots[slot, 3:6] = frac[:, lanes]
-
-
-def from_slots(place, pulled, out_pos, out_vel):
-    for b in range(place.shape[0]):
-        values = pulled[place[b]]
-        out_pos[:, b * LANES : (b + 1) * LANES] = values[:3]
-        out_vel[b : b + 1, :] = values[3:]
-
-
-def slot_rows(slots, i):
-    return [slots[i, r : r + 1] for r in range(6)]
+def thirds(values):
+    high = values.astype(BF16)
+    rest = values - high.astype(F32)
+    middle = rest.astype(BF16)
+    return [high, middle, (rest - middle.astype(F32)).astype(BF16)]
+
+
+def slot_matrix(dest, counts, los_size):
+    shape = (los_size, dest.shape[1])
+    slab = lax.broadcasted_iota(jnp.int32, shape, 0)
+    code = lax.broadcasted_iota(jnp.int32, shape, 1) * 256 + counts[...]
+    code = jnp.where(slab == dest[...], code, -1).astype(F32)
+    most = jnp.max(code, axis=1, keepdims=True)
+    least = jnp.min(jnp.where(code < 0.0, 65536.0, code), axis=1, keepdims=True)
+    single = least >= most
+    first = jnp.where(code == least, 1.0, 0.0)
+    second = jnp.where(single, 0.0, jnp.where(code == most, 1.0, 0.0))
+    matrix = jnp.concatenate([first, second], axis=0)
+    live = jnp.concatenate([jnp.maximum(least, 0.0), most], axis=0).astype(jnp.int32) & 255
+    some = jnp.concatenate([most >= 0.0, jnp.logical_not(single)], axis=0)
+    return matrix, jnp.where(some, live, 0)
+
+
+def slot_rows(slots, slot, t):
+    return [slots[slot, r, pl.ds(t, 1), :] for r in range(6)]
 
 
 def one_hot_deep(deep):
@@ -77,17 +65,30 @@
 
 
 def kernel(
+    dest_in,
+    counts_in,
+    cell_in,
+    frac_in,
+    off_in,
     bias_in,
     rsd_in,
-    slots,
     selection_in,
     galaxies_in,
-    pulled,
+    out_pos,
+    out_vel,
+    dest,
+    counts,
+    cell,
+    frac,
+    off,
     bias,
     rsd,
     selection,
     galaxies,
     fetch_sems,
+    rows_in,
+    slots,
+    pulled,
     hot,
     grid,
     grid_side,
@@ -117,6 +118,7 @@
 ):
     z_size = grid.shape[1]
     sky_size = lax.axis_size("sky")
+    los_size = X * z_size
     los_here = lax.axis_index("los")
     sky_here = lax.axis_index("sky")
     z_here = los_here // X
@@ -142,7 +144,19 @@
         pl.semaphore_signal(barrier, inc=1, device_id=(z_peer(k), sky_here), device_id_type=MESH)
 
     fetched = fetch(
-        (bias_in, rsd_in, selection_in, galaxies_in), (bias, rsd, selection, galaxies), fetch_sems
+        (
+            dest_in,
+            counts_in,
+            cell_in,
+            frac_in,
+            off_in,
+            bias_in,
+            rsd_in,
+            selection_in,
+            galaxies_in,
+        ),
+        (dest, counts, cell, frac, off, bias, rsd, selection, galaxies),
+        fetch_sems,
     )
     row4 = lax.broadcasted_iota(jnp.int32, (4, LANES), 0)
 
@@ -154,10 +168,39 @@
 
     row = row_iota().astype(F32)
 
+    for copy in fetched[:5]:
+        copy.wait()
+    blocks = dest.shape[1]
+    matrix, live = slot_matrix(dest, counts, los_size)
+    for b in range(blocks):
+        lanes = slice(b * LANES, (b + 1) * LANES)
+        cells = cell[:, lanes].astype(F32)
+        fracs = frac[:, lanes]
+        for r in range(3):
+            rows_in[r, b : b + 1, :] = cells[r : r + 1]
+            rows_in[3 + r, b : b + 1, :] = fracs[r : r + 1]
+    los_row = ((rows_in[0].astype(jnp.int32) + off[...]) & 3).astype(F32)
+    sky_row = rows_in[1] - (sky_here * 4).astype(F32)
+    parts = [los_row.astype(BF16), sky_row.astype(BF16), rows_in[2].astype(BF16)]
+    for r in range(3):
+        parts += thirds(rows_in[3 + r])
+    placed = jnp.dot(
+        matrix.astype(BF16), jnp.concatenate(parts, axis=1), preferred_element_type=F32
+    )
+    lane = lax.broadcasted_iota(jnp.int32, (2 * los_size, LANES), 1)
+    for r in range(6):
+        part = [placed[:, i * LANES : (i + 1) * LANES] for i in range(12)]
+        if r < 3:
+            value = jnp.where(lane < live, part[0], -8.0) if r == 0 else part[r]
+        else:
+            value = (part[3 * r - 6] + part[3 * r - 5]) + part[3 * r - 4]
+        for slot in (0, 1):
+            slots[slot, r] = value[slot * los_size : (slot + 1) * los_size]
+
     def paint(t):
         tables, hots = [], []
         for slot in (0, 1):
-            los, sky, deep, f_los, f_sky, f_deep = slot_rows(slots, t * 2 + slot)
+            los, sky, deep, f_los, f_sky, f_deep = slot_rows(slots, slot, t)
             h_los = jnp.where(row == los, 1.0 - f_los, 0.0) + jnp.where(row == los + 1, f_los, 0.0)
             h_sky = jnp.where(row == sky, 1.0 - f_sky, 0.0) + jnp.where(row == sky + 1, f_sky, 0.0)
             lower, upper = h_los * (1.0 - f_deep), h_los * f_deep
@@ -203,7 +246,7 @@
     before = lax.rem(z_here + order[-1], z_size)
     lax.fori_loop(0, z_size // 2, paint_step, tuple(paint(before * X + X - 1)))
 
-    for copy in fetched:
+    for copy in fetched[5:]:
         copy.wait()
     rates[x_here, z_here] = by_row(rsd)
     pl.semaphore_wait(barrier, 3 + 2 * X + z_size - 1)
@@ -361,7 +404,7 @@
         picked = picked[:80] + picked[80:]
         rate = jnp.concatenate([rates[x, z], jnp.zeros((4, LANES), F32)], axis=0)
         for slot in (0, 1):
-            los, sky, deep, f_los, f_sky, f_deep = slot_rows(slots, t * 2 + slot)
+            los, sky, deep, f_los, f_sky, f_deep = slot_rows(slots, slot, t)
             at, above = row == los, row == los + 1
             h_los = jnp.where(at, 1.0 - f_los, 0.0) + jnp.where(above, f_los, 0.0)
             d_los = jnp.where(above, 1.0, 0.0) - jnp.where(at, 1.0, 0.0)
@@ -382,7 +425,8 @@
             g_sky = jnp.sum(h_los * val_sky, axis=0, keepdims=True)
             g_deep = jnp.sum(h_los * val_deep, axis=0, keepdims=True)
             speed = jnp.sum(r_los, axis=0, keepdims=True) * g_los
-            pulled[t * 2 + slot] = jnp.concatenate([g_los, g_sky, g_deep, speed], axis=0)
+            for r, value in enumerate((g_los, g_sky, g_deep, speed)):
+                pulled[slot, r, pl.ds(t, 1), :] = value
 
     waited = set()
     for g in range(z_size // 2):
@@ -396,6 +440,19 @@
         for z in ((z_here + z_size - g - 1) % z_size, (z_here + g) % z_size):
             for x in range(X):
                 pull(z, x)
+
+    back = jnp.transpose(matrix).astype(BF16)
+    parts = []
+    for slot in (0, 1):
+        parts.append(jnp.concatenate([pulled[slot, r] for r in range(4)], axis=1))
+    result = jnp.dot(
+        jnp.concatenate([back] * 3, axis=1),
+        jnp.concatenate(thirds(jnp.concatenate(parts, axis=0)), axis=0),
+        preferred_element_type=F32,
+    )
+    for r in range(3):
+        out_pos[r] = result[:, r * LANES : (r + 1) * LANES]
+    out_vel[...] = result[:, 3 * LANES :]
 
     for copies in (
         x_copies,
@@ -426,39 +483,36 @@
     z_size = los_size // X
     blocks = block_dest.shape[0]
     vmem = pl.BlockSpec(memory_space=pltpu.VMEM)
-    smem = pl.BlockSpec(memory_space=pltpu.SMEM)
     hbm = pl.BlockSpec(memory_space=pltpu.HBM)
     dma = pltpu.SemaphoreType.DMA
-    slots, place = pl.pallas_call(
-        to_slots,
+    inputs = (
+        block_dest.reshape(1, blocks),
+        block_count.reshape(1, blocks),
+        part_cell,
+        part_frac,
+        los_offset.reshape(blocks, LANES),
+        bias_exp,
+        rsd_factor,
+        selection,
+        galaxy_counts,
+    )
+    grad_pos, grad_vel = pl.pallas_call(
+        kernel,
         out_shape=(
-            jax.ShapeDtypeStruct((2 * los_size, 8, LANES), F32),
-            jax.ShapeDtypeStruct((blocks,), jnp.int32),
+            jax.ShapeDtypeStruct((3, blocks, LANES), F32),
+            jax.ShapeDtypeStruct((blocks, LANES), F32),
         ),
-        in_specs=[hbm] * 5,
-        out_specs=(vmem, smem),
+        in_specs=[hbm] * len(inputs),
+        out_specs=(vmem, vmem),
         scratch_shapes=[
-            pltpu.SMEM((blocks,), jnp.int32),
-            pltpu.SMEM((blocks,), jnp.int32),
-            pltpu.VMEM(part_cell.shape, jnp.int32),
-            pltpu.VMEM(part_frac.shape, F32),
-            pltpu.VMEM((blocks, LANES), jnp.int32),
-            pltpu.SMEM((los_size,), jnp.int32),
-            dma((5,)),
-        ],
-        name="to_slots",
-    )(block_dest, block_count, part_cell, part_frac, los_offset.reshape(blocks, LANES))
-    pulled = pl.pallas_call(
-        kernel,
-        out_shape=jax.ShapeDtypeStruct((2 * los_size, 4, LANES), F32),
-        in_specs=[hbm, hbm, vmem, hbm, hbm],
-        out_specs=vmem,
-        scratch_shapes=[
-            pltpu.SMEM(bias_exp.shape, F32),
-            pltpu.SMEM(rsd_factor.shape, F32),
-            pltpu.VMEM(selection.shape, F32),
-            pltpu.VMEM(galaxy_counts.shape, jnp.int32),
-            dma((4,)),
+            *[
+                (pltpu.SMEM if value.ndim == 1 else pltpu.VMEM)(value.shape, value.dtype)
+                for value in inputs
+            ],
+            dma((len(inputs),)),
+            pltpu.VMEM((6, blocks, LANES), F32),
+            pltpu.VMEM((2, 6, los_size, LANES), F32),
+            pltpu.VMEM((2, 4, los_size, LANES), F32),
             pltpu.VMEM((los_size, LANES, 2 * LANES), BF16),
             pltpu.VMEM((X, z_size, 4, 4, LANES), F32),
             pltpu.VMEM((X, z_size, 4, LANES), F32),
@@ -490,18 +544,8 @@
             collective_id=0, has_side_effects=True
         ),
         name="adjoint",
-    )(bias_exp, rsd_factor, slots, selection, galaxy_counts)
-    grad_pos, grad_vel = pl.pallas_call(
-        from_slots,
-        out_shape=(
-            jax.ShapeDtypeStruct(part_frac.shape, F32),
-            jax.ShapeDtypeStruct((blocks, LANES), F32),
-        ),
-        in_specs=[smem, vmem],
-        out_specs=(vmem, vmem),
-        name="from_slots",
-    )(place, pulled)
-    return grad_pos, grad_vel.reshape(-1)
+    )(*inputs)
+    return grad_pos.reshape(3, -1), grad_vel.reshape(-1)
 
 
 def solution(mesh):

time: 40.1 us -> 38.7 us (0.965)
  Pallas kernels: 39.2 us -> 35.8 us
  local copies, waits for them, and re-layouts: 0 us -> 2.08 us
    pallas_call x3 -> x1, Pallas kernels: 39.2 us -> 35.8 us  [on_device(): pl.pallas_call(kernel, out_shape=(jax.ShapeDtypeStruct((3, blocks, LANES)...]
    unnamed x0 -> x4, local copies, waits for them, and re-layouts: none -> 2.08 us
where the time goes in v3:
time: 38.7 us; the launch traced here: 38.5 us
  Pallas kernels  35.8 us (93%)
  local copies, waits for them, and re-layouts  2.08 us (5%)
  between operations  0.65 us (2%)
    pallas_call x1, Pallas kernels, on_device(): pl.pallas_call(kernel, out_shape=(jax.ShapeDtypeStruct((3, blocks, LANES)...  35.8 us
    unnamed x4, local copies, waits for them, and re-layouts  2.08 us

profile of v3, /device:TPU:25, one launch (start us, length us, event | category | flops | bytes accessed | tf_op | source)
XLA Modules:
  0.0 38.5 jit_solution(108607742567070583)
XLA Ops:
  0.6 35.8 %adjoint.1 = (f32[3,32,128]{2,1,0:T(8,128)}, f32[32,128]{1,0:T(8,128)}) custom-call(s32[1,32]{1,0:T(1,128)} %bitcast.12, s32[1,32]{1,0:T(1,128)} %bitcast.13, s32[3,4096]{1,0:T(4,128)} %cell_in.1, f32[3,4096]{1,0:T(4,128)} %frac_in.1, s32[32,128]{1,0:T(8,128)} %bitcast.11, f32[4]{0:T(128)} %bias_in.1, f32[4]{0:T(128)} %rsd_in.1, f32[4,4,128]{2,1,0:T(4,128)} %selection_in.1, ...), custom_call_target="tpu_custom_call" | custom-call | tf_op jit(solution)/shard_map/adjoint/pallas_call | solution.py:499
  36.4 0.0 copy-start
  36.4 1.5 %copy.13 = f32[1,3,32,128]{3,1,2,0:T(4,128)} copy(f32[1,3,32,128]{3,2,1,0:T(8,128)} %bitcast.9) | data formatting | bytes 98304
  37.9 0.0 copy-done
  37.9 0.6 %copy.15 = f32[4096]{0:T(1024)} copy(f32[4096]{0:T(1024)S(1)} %bitcast.10) | data formatting | bytes 32768
Async XLA Ops:
  36.4 1.5 %copy-start = (f32[32,128]{1,0:T(8,128)S(1)}, f32[32,128]{1,0:T(8,128)}, u32[]{:S(2)}) copy-start(f32[32,128]{1,0:T(8,128)} %get-tuple-element.5) | copy-start | bytes 49156

commit v4 on v3

--- a/solution.py
+++ b/solution.py
@@ -99,22 +99,12 @@
     field,
     field_side,
     rates,
-    send_x,
+    send_sems,
     recv_x,
-    send_side,
-    recv_side,
-    send_z,
     recv_z,
-    send_cz,
     recv_cz,
-    send_f,
     recv_f,
-    send_fs,
-    recv_fs,
-    send_rz,
-    recv_rz,
-    send_rx,
-    recv_rx,
+    recv_rates,
 ):
     z_size = grid.shape[1]
     sky_size = lax.axis_size("sky")
@@ -131,17 +121,6 @@
 
     def z_peer(k):
         return ((z_here + k) % z_size) * X + x_here
-
-    barrier = pltpu.get_barrier_semaphore()
-    for k in range(X):
-        if k:
-            pl.semaphore_signal(
-                barrier, inc=1, device_id=(x_peer(k), sky_here), device_id_type=MESH
-            )
-        for sky_to in (sky_up, sky_down):
-            pl.semaphore_signal(barrier, inc=1, device_id=(x_peer(k), sky_to), device_id_type=MESH)
-    for k in range(1, z_size):
-        pl.semaphore_signal(barrier, inc=1, device_id=(z_peer(k), sky_here), device_id_type=MESH)
 
     fetched = fetch(
         (
@@ -158,6 +137,17 @@
         (dest, counts, cell, frac, off, bias, rsd, selection, galaxies),
         fetch_sems,
     )
+    barrier = pltpu.get_barrier_semaphore()
+    for k in range(X):
+        if k:
+            pl.semaphore_signal(
+                barrier, inc=1, device_id=(x_peer(k), sky_here), device_id_type=MESH
+            )
+        for sky_to in (sky_up, sky_down):
+            pl.semaphore_signal(barrier, inc=1, device_id=(x_peer(k), sky_to), device_id_type=MESH)
+    for k in range(1, z_size):
+        pl.semaphore_signal(barrier, inc=1, device_id=(z_peer(k), sky_here), device_id_type=MESH)
+
     row4 = lax.broadcasted_iota(jnp.int32, (4, LANES), 0)
 
     def by_row(scalars):
@@ -226,6 +216,19 @@
 
     order = [(z_size // 2 - 1 + j) % z_size for j in range(z_size)]
 
+    def remote(src, dst, send_sem, recv_sem, los_to, sky_to):
+        return pltpu.make_async_remote_copy(
+            src_ref=src,
+            dst_ref=dst,
+            send_sem=send_sem,
+            recv_sem=recv_sem,
+            device_id=(los_to, sky_to),
+            device_id_type=MESH,
+        )
+
+    def wait_for(ref, sem):
+        pltpu.make_async_copy(ref, ref, sem).wait()
+
     def paint_step(step, previous):
         for i in range(2):
             j = step * 2 + i
@@ -240,6 +243,31 @@
                     else:
                         grid_side[x, j] = whole
                 previous = planes
+
+        @pl.when(step == 0)
+        def _():
+            pl.semaphore_wait(barrier, 3 + 2 * X + z_size - 1)
+
+        part = pl.ds(step * 2, 2)
+        for k in (2, 1, 3, 0):
+            x_to = (x_here + k) % X
+            if k:
+                remote(
+                    grid.at[x_to, part],
+                    rx.at[k - 1, part],
+                    send_sems.at[0],
+                    recv_x.at[step],
+                    x_peer(k),
+                    sky_here,
+                ).start()
+            remote(
+                grid_side.at[x_to, part],
+                rx_side.at[k, part],
+                send_sems.at[0],
+                recv_x.at[step],
+                x_peer(k),
+                sky_up,
+            ).start()
         return tuple(previous)
 
     zero = jnp.zeros((8, LANES), F32)
@@ -249,60 +277,13 @@
     for copy in fetched[5:]:
         copy.wait()
     rates[x_here, z_here] = by_row(rsd)
-    pl.semaphore_wait(barrier, 3 + 2 * X + z_size - 1)
-
-    def remote(src, dst, send_sem, recv_sem, los_to, sky_to):
-        return pltpu.make_async_remote_copy(
-            src_ref=src,
-            dst_ref=dst,
-            send_sem=send_sem,
-            recv_sem=recv_sem,
-            device_id=(los_to, sky_to),
-            device_id_type=MESH,
-        )
-
-    groups = [range(i, i + 2) for i in range(0, z_size, 2)]
-    x_copies, side_copies, z_copies, rate_z = {}, {}, {}, {}
-    for g, group in enumerate(groups):
-        part = pl.ds(group[0], len(group))
-        for k in (2, 1, 3, 0):
-            x_to = (x_here + k) % X
-            if k:
-                x_copies[g, k] = remote(
-                    grid.at[x_to, part],
-                    rx.at[k - 1, part],
-                    send_x.at[g, k - 1],
-                    recv_x.at[g, k - 1],
-                    x_peer(k),
-                    sky_here,
-                )
-                x_copies[g, k].start()
-            side_copies[g, k] = remote(
-                grid_side.at[x_to, part],
-                rx_side.at[k, part],
-                send_side.at[g, k],
-                recv_side.at[g, k],
-                x_peer(k),
-                sky_up,
-            )
-            side_copies[g, k].start()
     for k in range(1, z_size):
-        rate_z[k] = remote(
-            rates.at[x_here, z_here],
-            rates.at[x_here, z_here],
-            send_rz.at[k - 1],
-            recv_rz.at[k - 1],
-            z_peer(k),
-            sky_here,
-        )
-        rate_z[k].start()
-
-    for g, group in enumerate(groups):
-        for k in range(X):
-            if k:
-                x_copies[g, k].wait_recv()
-            side_copies[g, k].wait_recv()
-        for j in group:
+        here = rates.at[x_here, z_here]
+        remote(here, here, send_sems.at[1], recv_rates.at[0], z_peer(k), sky_here).start()
+
+    for g in range(z_size // 2):
+        wait_for(grid.at[:, pl.ds(2 * g, 2)], recv_x.at[g])
+        for j in (2 * g, 2 * g + 1):
             for s in range(4):
                 value = grid[x_here, j, s]
                 for k in range(1, X):
@@ -313,33 +294,17 @@
                 total[j, s] = value
             k = order[j]
             if k:
-                z_copies[k] = remote(
-                    total.at[j],
-                    rz.at[k - 1],
-                    send_z.at[k - 1],
-                    recv_z.at[k - 1],
-                    z_peer(k),
-                    sky_here,
-                )
-                z_copies[k].start()
-
-    for k in range(1, z_size):
-        rate_z[k].wait_recv()
-    rate_x = {}
+                remote(
+                    total.at[j], rz.at[k - 1], send_sems.at[2], recv_z, z_peer(k), sky_here
+                ).start()
+
+    wait_for(rates.at[0, pl.ds(0, z_size - 1)], recv_rates.at[0])
     for k in range(1, X):
-        rate_x[k] = remote(
-            rates.at[x_here],
-            rates.at[x_here],
-            send_rx.at[k - 1],
-            recv_rx.at[k - 1],
-            x_peer(k),
-            sky_here,
-        )
-        rate_x[k].start()
+        here = rates.at[x_here]
+        remote(here, here, send_sems.at[3], recv_rates.at[1], x_peer(k), sky_here).start()
 
     exponent = by_row(bias)
-    for k in range(1, z_size):
-        z_copies[k].wait_recv()
+    wait_for(rz, recv_z)
     for s in range(4):
         density = total[order.index(0), s]
         for k in range(1, z_size):
@@ -350,44 +315,38 @@
         intensity = mean * jnp.exp(exponent * jnp.log(shifted))
         field[x_here, z_here, s] = (1.0 - seen / intensity) * exponent * intensity / shifted
 
-    cz_copies = {}
-    for k in sorted(range(1, z_size), key=lambda k: -min(k, z_size - k)):
-        cz_copies[k] = remote(
-            field.at[x_here, z_here],
-            field.at[x_here, z_here],
-            send_cz.at[k - 1],
-            recv_cz.at[k - 1],
-            z_peer(k),
-            sky_here,
-        )
-        cz_copies[k].start()
-    f_copies, fs_copies = {}, {}
-    for j in sorted(range(z_size), key=lambda k: min(k, z_size - k)):
-        if j:
-            cz_copies[j].wait_recv()
+    def ring_distance(j):
+        return min(j, z_size - j)
+
+    nearest = sorted(range(z_size), key=ring_distance)
+    for k in nearest[1:]:
+        here = field.at[x_here, z_here]
+        remote(
+            here, here, send_sems.at[4], recv_cz.at[ring_distance(k) - 1], z_peer(k), sky_here
+        ).start()
+    arrived = {0}
+    for j in nearest:
+        if ring_distance(j) not in arrived:
+            arrived.add(ring_distance(j))
+            pieces = 1 if 2 * j == z_size else 2
+            wait_for(rz.at[pl.ds(0, pieces)], recv_cz.at[ring_distance(j) - 1])
         z_from = (z_here + z_size - j) % z_size
         for k in (2, 1, 3, 0):
             if k:
-                f_copies[j, k] = remote(
-                    field.at[x_here, z_from],
-                    field.at[x_here, z_from],
-                    send_f.at[j, k - 1],
-                    recv_f.at[j, k - 1],
-                    x_peer(k),
-                    sky_here,
-                )
-                f_copies[j, k].start()
-            fs_copies[j, k] = remote(
+                here = field.at[x_here, z_from]
+                remote(
+                    here, here, send_sems.at[5], recv_f.at[ring_distance(j)], x_peer(k), sky_here
+                ).start()
+            remote(
                 field.at[x_here, z_from, 0],
                 field_side.at[x_here, z_from],
-                send_fs.at[j, k],
-                recv_fs.at[j, k],
+                send_sems.at[5],
+                recv_f.at[ring_distance(j)],
                 x_peer(k),
                 sky_down,
-            )
-            fs_copies[j, k].start()
-    for k in range(1, X):
-        rate_x[k].wait_recv()
+            ).start()
+    wait_for(rates.at[pl.ds(0, X - 1)], recv_rates.at[1])
+
     def pull(z, x):
         t = z * X + x
         z_next, x_next = (z, x + 1) if x + 1 < X else ((z + 1) % z_size, 0)
@@ -428,15 +387,11 @@
             for r, value in enumerate((g_los, g_sky, g_deep, speed)):
                 pulled[slot, r, pl.ds(t, 1), :] = value
 
-    waited = set()
     for g in range(z_size // 2):
-        for j in (0, g + 1, z_size - g - 1):
-            if j not in waited:
-                waited.add(j)
-                for k in range(X):
-                    if k:
-                        f_copies[j, k].wait_recv()
-                    fs_copies[j, k].wait_recv()
+        if g == 0:
+            wait_for(grid.at[:, 0], recv_f.at[0])
+        pieces = 1 if g + 1 == z_size // 2 else 2
+        wait_for(grid.at[:, pl.ds(0, pieces)], recv_f.at[g + 1])
         for z in ((z_here + z_size - g - 1) % z_size, (z_here + g) % z_size):
             for x in range(X):
                 pull(z, x)
@@ -450,22 +405,17 @@
         jnp.concatenate(thirds(jnp.concatenate(parts, axis=0)), axis=0),
         preferred_element_type=F32,
     )
-    for r in range(3):
-        out_pos[r] = result[:, r * LANES : (r + 1) * LANES]
+    for b in range(blocks):
+        for r in range(3):
+            out_pos[r : r + 1, b * LANES : (b + 1) * LANES] = result[
+                b : b + 1, r * LANES : (r + 1) * LANES
+            ]
     out_vel[...] = result[:, 3 * LANES :]
 
-    for copies in (
-        x_copies,
-        side_copies,
-        rate_z,
-        z_copies,
-        rate_x,
-        cz_copies,
-        f_copies,
-        fs_copies,
+    for sent, ref in enumerate(
+        (grid, rates.at[0, pl.ds(0, z_size - 1)], rz, rates.at[pl.ds(0, X - 1)], rz, grid)
     ):
-        for copy in copies.values():
-            copy.wait_send()
+        wait_for(ref, send_sems.at[sent])
 
 
 def on_device(
@@ -499,8 +449,8 @@
     grad_pos, grad_vel = pl.pallas_call(
         kernel,
         out_shape=(
-            jax.ShapeDtypeStruct((3, blocks, LANES), F32),
-            jax.ShapeDtypeStruct((blocks, LANES), F32),
+            pltpu.VMEM(part_frac.shape, F32),
+            pltpu.VMEM((blocks, LANES), F32),
         ),
         in_specs=[hbm] * len(inputs),
         out_specs=(vmem, vmem),
@@ -523,29 +473,19 @@
             pltpu.VMEM((X, z_size, 4, 4, LANES), F32),
             pltpu.VMEM((X, z_size, 4, LANES), F32),
             pltpu.VMEM((X, z_size, 4, LANES), F32),
-            dma((z_size // 2, X - 1)),
-            dma((z_size // 2, X - 1)),
-            dma((z_size // 2, X)),
-            dma((z_size // 2, X)),
-            dma((z_size - 1,)),
-            dma((z_size - 1,)),
-            dma((z_size - 1,)),
-            dma((z_size - 1,)),
-            dma((z_size, X - 1)),
-            dma((z_size, X - 1)),
-            dma((z_size, X)),
-            dma((z_size, X)),
-            dma((z_size - 1,)),
-            dma((z_size - 1,)),
-            dma((X - 1,)),
-            dma((X - 1,)),
+            dma((6,)),
+            dma((z_size // 2,)),
+            dma,
+            dma((z_size // 2,)),
+            dma((z_size // 2 + 1,)),
+            dma((2,)),
         ],
         compiler_params=pltpu.CompilerParams(
             collective_id=0, has_side_effects=True
         ),
         name="adjoint",
     )(*inputs)
-    return grad_pos.reshape(3, -1), grad_vel.reshape(-1)
+    return grad_pos, grad_vel.reshape(-1)
 
 
 def solution(mesh):

time: 38.7 us -> 35.3 us (0.912)
  Pallas kernels: 35.8 us -> 33.2 us
  local copies, waits for them, and re-layouts: 2.08 us -> 1.24 us
    pallas_call x1, Pallas kernels: 35.8 us -> 33.2 us  [on_device(): pl.pallas_call(kernel, out_shape=(pltpu.VMEM(part_frac.shape, F32), pltpu...]
    unnamed x4 -> x2, local copies, waits for them, and re-layouts: 2.08 us -> 1.24 us
where the time goes in v4:
time: 35.3 us; the launch traced here: 35.1 us
  Pallas kernels  33.2 us (94%)
  local copies, waits for them, and re-layouts  1.24 us (4%)
  between operations  0.64 us (2%)
    pallas_call x1, Pallas kernels, on_device(): pl.pallas_call(kernel, out_shape=(pltpu.VMEM(part_frac.shape, F32), pltpu...  33.2 us
    unnamed x2, local copies, waits for them, and re-layouts  1.24 us

profile of v4, /device:TPU:25, one launch (start us, length us, event | category | flops | bytes accessed | tf_op | source)
XLA Modules:
  0.0 35.1 jit_solution(9775468875074578582)
XLA Ops:
  0.6 33.2 %adjoint.1 = (f32[3,4096]{1,0:T(4,128)S(1)}, f32[32,128]{1,0:T(8,128)S(1)}) custom-call(s32[1,32]{1,0:T(1,128)} %bitcast.6, s32[1,32]{1,0:T(1,128)} %bitcast.7, s32[3,4096]{1,0:T(4,128)} %cell_in.1, f32[3,4096]{1,0:T(4,128)} %frac_in.1, s32[32,128]{1,0:T(8,128)} %bitcast.5, f32[4]{0:T(128)} %bias_in.1, f32[4]{0:T(128)} %rsd_in.1, f32[4,4,128]{2,1,0:T(4,128)} %selection_in.1, ...), custom_call_target="tpu_custom_call" | custom-call | tf_op jit(solution)/shard_map/adjoint/pallas_call | solution.py:449
  33.9 0.6 %copy.13 = f32[3,4096]{1,0:T(4,128)} copy(f32[3,4096]{1,0:T(4,128)S(1)} %get-tuple-element.6) | data formatting | bytes 98304
  34.5 0.6 %copy.14 = f32[4096]{0:T(1024)} copy(f32[4096]{0:T(1024)S(1)} %bitcast.4) | data formatting | bytes 32768

commit v5 on v4

--- a/solution.py
+++ b/solution.py
@@ -60,8 +60,9 @@
 
 
 def one_hot_deep(deep):
-    iota = lax.broadcasted_iota(jnp.int32, (LANES, LANES), 0).astype(F32)
-    return jnp.where(iota == deep, 1.0, 0.0).astype(BF16)
+    iota = lax.broadcasted_iota(jnp.int32, (LANES, LANES), 0).astype(F32).astype(BF16)
+    one, none = jnp.ones((), BF16), jnp.zeros((), BF16)
+    return jnp.where(iota == deep.astype(BF16), one, none)
 
 
 def kernel(
@@ -89,7 +90,6 @@
     rows_in,
     slots,
     pulled,
-    hot,
     grid,
     grid_side,
     rx,
@@ -198,9 +198,7 @@
             for s in range(5):
                 parts += [h_sky[s : s + 1] * lower, h_sky[s : s + 1] * upper]
             tables.append(split(jnp.concatenate(parts, axis=0)))
-            one_hot = one_hot_deep(deep)
-            hot[t, :, slot * LANES : (slot + 1) * LANES] = one_hot
-            hots.append(one_hot)
+            hots.append(one_hot_deep(deep))
         result = lax.dot_general(
             jnp.concatenate(tables, axis=1),
             jnp.concatenate(hots, axis=1),
@@ -229,25 +227,7 @@
     def wait_for(ref, sem):
         pltpu.make_async_copy(ref, ref, sem).wait()
 
-    def paint_step(step, previous):
-        for i in range(2):
-            j = step * 2 + i
-            z = lax.rem(z_here + order[0] + j, z_size)
-            for x in range(X):
-                planes = paint(z * X + x)
-                for s in range(5):
-                    carried = jnp.where(row == 0, pltpu.roll(previous[s], 4, 0), 0.0)
-                    whole = (planes[s] + carried)[:4]
-                    if s < 4:
-                        grid[x, j, s] = whole
-                    else:
-                        grid_side[x, j] = whole
-                previous = planes
-
-        @pl.when(step == 0)
-        def _():
-            pl.semaphore_wait(barrier, 3 + 2 * X + z_size - 1)
-
+    def send_group(step):
         part = pl.ds(step * 2, 2)
         for k in (2, 1, 3, 0):
             x_to = (x_here + k) % X
@@ -268,6 +248,31 @@
                 x_peer(k),
                 sky_up,
             ).start()
+
+    def paint_step(step, previous):
+        for i in range(2):
+            j = step * 2 + i
+            z = lax.rem(z_here + order[0] + j, z_size)
+            for x in range(X):
+                planes = paint(z * X + x)
+                for s in range(5):
+                    carried = jnp.where(row == 0, pltpu.roll(previous[s], 4, 0), 0.0)
+                    whole = (planes[s] + carried)[:4]
+                    if s < 4:
+                        grid[x, j, s] = whole
+                    else:
+                        grid_side[x, j] = whole
+                previous = planes
+
+        @pl.when(step == 1)
+        def _():
+            pl.semaphore_wait(barrier, 3 + 2 * X + z_size - 1)
+            send_group(0)
+
+        @pl.when(step >= 1)
+        def _():
+            send_group(step)
+
         return tuple(previous)
 
     zero = jnp.zeros((8, LANES), F32)
@@ -357,13 +362,16 @@
             else:
                 value = jnp.concatenate([field_side[x, z], field_side[x_next, z_next]], axis=0)
             rows += [value, pltpu.roll(value, LANES - 1, 1)]
+        both = [slot_rows(slots, slot, t) for slot in (0, 1)]
         picked = jnp.dot(
-            split(jnp.concatenate(rows, axis=0)), hot[t], preferred_element_type=F32
+            split(jnp.concatenate(rows, axis=0)),
+            jnp.concatenate([one_hot_deep(values[2]) for values in both], axis=1),
+            preferred_element_type=F32,
         )
         picked = picked[:80] + picked[80:]
         rate = jnp.concatenate([rates[x, z], jnp.zeros((4, LANES), F32)], axis=0)
         for slot in (0, 1):
-            los, sky, deep, f_los, f_sky, f_deep = slot_rows(slots, slot, t)
+            los, sky, deep, f_los, f_sky, f_deep = both[slot]
             at, above = row == los, row == los + 1
             h_los = jnp.where(at, 1.0 - f_los, 0.0) + jnp.where(above, f_los, 0.0)
             d_los = jnp.where(above, 1.0, 0.0) - jnp.where(at, 1.0, 0.0)
@@ -392,9 +400,11 @@
             wait_for(grid.at[:, 0], recv_f.at[0])
         pieces = 1 if g + 1 == z_size // 2 else 2
         wait_for(grid.at[:, pl.ds(0, pieces)], recv_f.at[g + 1])
-        for z in ((z_here + z_size - g - 1) % z_size, (z_here + g) % z_size):
-            for x in range(X):
-                pull(z, x)
+        ready = [(z_size - g - 1, x) for x in range(X)] + [(g, X - 1)]
+        for d in {0: (0, 1), z_size // 2 - 1: ()}.get(g, (g + 1,)):
+            ready += [(d, x) for x in range(X - 1)]
+        for d, x in ready:
+            pull((z_here + d) % z_size, x)
 
     back = jnp.transpose(matrix).astype(BF16)
     parts = []
@@ -416,6 +426,11 @@
         (grid, rates.at[0, pl.ds(0, z_size - 1)], rz, rates.at[pl.ds(0, X - 1)], rz, grid)
     ):
         wait_for(ref, send_sems.at[sent])
+
+
+def write_out(pos, vel, out_pos, out_vel, sems):
+    for copy in fetch((pos, vel), (out_pos, out_vel), sems):
+        copy.wait()
 
 
 def on_device(
@@ -463,7 +478,6 @@
             pltpu.VMEM((6, blocks, LANES), F32),
             pltpu.VMEM((2, 6, los_size, LANES), F32),
             pltpu.VMEM((2, 4, los_size, LANES), F32),
-            pltpu.VMEM((los_size, LANES, 2 * LANES), BF16),
             pltpu.VMEM((X, z_size, 4, 4, LANES), F32),
             pltpu.VMEM((X, z_size, 4, LANES), F32),
             pltpu.VMEM((X - 1, z_size, 4, 4, LANES), F32),
@@ -485,6 +499,18 @@
         ),
         name="adjoint",
     )(*inputs)
+    grad_pos, grad_vel = pl.pallas_call(
+        write_out,
+        out_shape=(
+            jax.ShapeDtypeStruct(grad_pos.shape, F32),
+            jax.ShapeDtypeStruct(grad_vel.shape, F32),
+        ),
+        in_specs=[vmem, vmem],
+        out_specs=(hbm, hbm),
+        scratch_shapes=[dma((2,))],
+        compiler_params=pltpu.CompilerParams(vmem_limit_bytes=1 << 20),
+        name="write_out",
+    )(grad_pos, grad_vel)
     return grad_pos, grad_vel.reshape(-1)
 
 

time: 35.3 us -> 34.3 us (0.972)
  local copies, waits for them, and re-layouts: 1.24 us -> 0 us
    unnamed x2 -> x0, local copies, waits for them, and re-layouts: 1.24 us -> none
    pallas_call x0 -> x1, Pallas kernels: none -> 0.65 us  [on_device(): pl.pallas_call(write_out, out_shape=(jax.ShapeDtypeStruct(grad_pos.shape,...]
where the time goes in v5:
time: 34.3 us; the launch traced here: 34.2 us
  Pallas kernels  33.5 us (98%)
  between operations  0.64 us (2%)
    pallas_call x1, Pallas kernels, on_device(): pl.pallas_call(kernel, out_shape=(pltpu.VMEM(part_frac.shape, F32), pltpu...  32.9 us

profile of v5, /device:TPU:25, one launch (start us, length us, event | category | flops | bytes accessed | tf_op | source)
XLA Modules:
  0.0 34.2 jit_solution(8748911606742974908)
XLA Ops:
  0.6 32.9 %adjoint.1 = (f32[3,4096]{1,0:T(4,128)S(1)}, f32[32,128]{1,0:T(8,128)S(1)}) custom-call(s32[1,32]{1,0:T(1,128)} %bitcast.5, s32[1,32]{1,0:T(1,128)} %bitcast.6, s32[3,4096]{1,0:T(4,128)} %cell_in.1, f32[3,4096]{1,0:T(4,128)} %frac_in.1, s32[32,128]{1,0:T(8,128)} %bitcast.4, f32[4]{0:T(128)} %bias_in.1, f32[4]{0:T(128)} %rsd_in.1, f32[4,4,128]{2,1,0:T(4,128)} %selection_in.1, ...), custom_call_target="tpu_custom_call" | custom-call | tf_op jit(solution)/shard_map/adjoint/pallas_call | solution.py:464
  33.5 0.7 %write_out.1 = (f32[3,4096]{1,0:T(4,128)}, f32[32,128]{1,0:T(8,128)}) custom-call(f32[3,4096]{1,0:T(4,128)S(1)} %get-tuple-element.6.pos, f32[32,128]{1,0:T(8,128)S(1)} %get-tuple-element.7.vel), custom_call_target="tpu_custom_call" | custom-call | tf_op jit(solution)/shard_map/write_out/pallas_call | solution.py:502

commit v6 on v5

--- a/solution.py
+++ b/solution.py
@@ -212,7 +212,7 @@
             planes.append(lower + pltpu.roll(upper, 1, 1))
         return planes
 
-    order = [(z_size // 2 - 1 + j) % z_size for j in range(z_size)]
+    order = [(z_size // 2 - 2 + j) % z_size for j in range(z_size)]
 
     def remote(src, dst, send_sem, recv_sem, los_to, sky_to):
         return pltpu.make_async_remote_copy(
@@ -264,15 +264,11 @@
                         grid_side[x, j] = whole
                 previous = planes
 
-        @pl.when(step == 1)
+        @pl.when(step == 0)
         def _():
             pl.semaphore_wait(barrier, 3 + 2 * X + z_size - 1)
-            send_group(0)
-
-        @pl.when(step >= 1)
-        def _():
-            send_group(step)
-
+
+        send_group(step)
         return tuple(previous)
 
     zero = jnp.zeros((8, LANES), F32)
@@ -323,33 +319,47 @@
     def ring_distance(j):
         return min(j, z_size - j)
 
-    nearest = sorted(range(z_size), key=ring_distance)
-    for k in nearest[1:]:
-        here = field.at[x_here, z_here]
-        remote(
-            here, here, send_sems.at[4], recv_cz.at[ring_distance(k) - 1], z_peer(k), sky_here
-        ).start()
-    arrived = {0}
-    for j in nearest:
-        if ring_distance(j) not in arrived:
-            arrived.add(ring_distance(j))
-            pieces = 1 if 2 * j == z_size else 2
-            wait_for(rz.at[pl.ds(0, pieces)], recv_cz.at[ring_distance(j) - 1])
-        z_from = (z_here + z_size - j) % z_size
+    def send_z(distance):
+        for k in sorted({distance, z_size - distance}):
+            here = field.at[x_here, z_here]
+            remote(
+                here, here, send_sems.at[4], recv_cz.at[distance - 1], z_peer(k), sky_here
+            ).start()
+
+    def send_x(distance, z_from, z_to):
         for k in (2, 1, 3, 0):
+            los_to = z_to * X + (x_here + k) % X
             if k:
                 here = field.at[x_here, z_from]
                 remote(
-                    here, here, send_sems.at[5], recv_f.at[ring_distance(j)], x_peer(k), sky_here
+                    here, here, send_sems.at[5], recv_f.at[distance], los_to, sky_here
                 ).start()
             remote(
                 field.at[x_here, z_from, 0],
                 field_side.at[x_here, z_from],
                 send_sems.at[5],
-                recv_f.at[ring_distance(j)],
-                x_peer(k),
+                recv_f.at[distance],
+                los_to,
                 sky_down,
             ).start()
+
+    def wait_z(distance):
+        pieces = 1 if 2 * distance == z_size else 2
+        wait_for(rz.at[pl.ds(0, pieces)], recv_cz.at[distance - 1])
+
+    straight = range(1, 2)
+    passed_on = range(2, z_size // 2 + 1)
+    for distance in passed_on:
+        send_z(distance)
+    send_x(0, z_here, z_here)
+    for distance in straight:
+        send_z(distance)
+        for k in (distance, z_size - distance):
+            send_x(distance, z_here, (z_here + k) % z_size)
+    for distance in passed_on:
+        wait_z(distance)
+        for k in sorted({distance, z_size - distance}):
+            send_x(distance, (z_here + k) % z_size, z_here)
     wait_for(rates.at[pl.ds(0, X - 1)], recv_rates.at[1])
 
     def pull(z, x):
@@ -398,6 +408,8 @@
     for g in range(z_size // 2):
         if g == 0:
             wait_for(grid.at[:, 0], recv_f.at[0])
+        if g + 1 in straight:
+            wait_z(g + 1)
         pieces = 1 if g + 1 == z_size // 2 else 2
         wait_for(grid.at[:, pl.ds(0, pieces)], recv_f.at[g + 1])
         ready = [(z_size - g - 1, x) for x in range(X)] + [(g, X - 1)]

time: 34.3 us -> 33.6 us (0.980)
  Pallas kernels: 33.5 us -> 32.8 us
    pallas_call x1, Pallas kernels: 32.9 us -> 32.1 us  [on_device(): pl.pallas_call(kernel, out_shape=(pltpu.VMEM(part_frac.shape, F32), pltpu...]
where the time goes in v6:
time: 33.6 us; the launch traced here: 33.4 us
  Pallas kernels  32.8 us (98%)
  between operations  0.64 us (2%)
    pallas_call x1, Pallas kernels, on_device(): pl.pallas_call(kernel, out_shape=(pltpu.VMEM(part_frac.shape, F32), pltpu...  32.1 us

profile of v6, /device:TPU:25, one launch (start us, length us, event | category | flops | bytes accessed | tf_op | source)
XLA Modules:
  0.0 33.4 jit_solution(10353368280361475577)
XLA Ops:
  0.6 32.1 %adjoint.1 = (f32[3,4096]{1,0:T(4,128)S(1)}, f32[32,128]{1,0:T(8,128)S(1)}) custom-call(s32[1,32]{1,0:T(1,128)} %bitcast.5, s32[1,32]{1,0:T(1,128)} %bitcast.6, s32[3,4096]{1,0:T(4,128)} %cell_in.1, f32[3,4096]{1,0:T(4,128)} %frac_in.1, s32[32,128]{1,0:T(8,128)} %bitcast.4, f32[4]{0:T(128)} %bias_in.1, f32[4]{0:T(128)} %rsd_in.1, f32[4,4,128]{2,1,0:T(4,128)} %selection_in.1, ...), custom_call_target="tpu_custom_call" | custom-call | tf_op jit(solution)/shard_map/adjoint/pallas_call | solution.py:476
  32.8 0.7 %write_out.1 = (f32[3,4096]{1,0:T(4,128)}, f32[32,128]{1,0:T(8,128)}) custom-call(f32[3,4096]{1,0:T(4,128)S(1)} %get-tuple-element.6.pos, f32[32,128]{1,0:T(8,128)S(1)} %get-tuple-element.7.vel), custom_call_target="tpu_custom_call" | custom-call | tf_op jit(solution)/shard_map/write_out/pallas_call | solution.py:514

commit v7 on v6

--- a/solution.py
+++ b/solution.py
@@ -191,8 +191,8 @@
         tables, hots = [], []
         for slot in (0, 1):
             los, sky, deep, f_los, f_sky, f_deep = slot_rows(slots, slot, t)
-            h_los = jnp.where(row == los, 1.0 - f_los, 0.0) + jnp.where(row == los + 1, f_los, 0.0)
-            h_sky = jnp.where(row == sky, 1.0 - f_sky, 0.0) + jnp.where(row == sky + 1, f_sky, 0.0)
+            h_los = jnp.where(row == los, 1.0 - f_los, jnp.where(row == los + 1, f_los, 0.0))
+            h_sky = jnp.where(row == sky, 1.0 - f_sky, jnp.where(row == sky + 1, f_sky, 0.0))
             lower, upper = h_los * (1.0 - f_deep), h_los * f_deep
             parts = []
             for s in range(5):
@@ -271,7 +271,6 @@
         send_group(step)
         return tuple(previous)
 
-    zero = jnp.zeros((8, LANES), F32)
     before = lax.rem(z_here + order[-1], z_size)
     lax.fori_loop(0, z_size // 2, paint_step, tuple(paint(before * X + X - 1)))
 
@@ -327,19 +326,19 @@
             ).start()
 
     def send_x(distance, z_from, z_to):
+        for k in (2, 1, 3):
+            here = field.at[x_here, z_from]
+            los_to = z_to * X + (x_here + k) % X
+            remote(here, here, send_sems.at[5], recv_f.at[distance], los_to, sky_here).start()
+
+    def send_side(distance, z_from, z_to):
         for k in (2, 1, 3, 0):
-            los_to = z_to * X + (x_here + k) % X
-            if k:
-                here = field.at[x_here, z_from]
-                remote(
-                    here, here, send_sems.at[5], recv_f.at[distance], los_to, sky_here
-                ).start()
             remote(
                 field.at[x_here, z_from, 0],
                 field_side.at[x_here, z_from],
                 send_sems.at[5],
                 recv_f.at[distance],
-                los_to,
+                z_to * X + (x_here + k) % X,
                 sky_down,
             ).start()
 
@@ -348,10 +347,15 @@
         wait_for(rz.at[pl.ds(0, pieces)], recv_cz.at[distance - 1])
 
     straight = range(1, 2)
+    straight_sides = (4, 3, 2, 1)
     passed_on = range(2, z_size // 2 + 1)
     for distance in passed_on:
         send_z(distance)
     send_x(0, z_here, z_here)
+    for distance in straight_sides:
+        for k in sorted({distance, z_size - distance}):
+            send_side(distance, z_here, (z_here + k) % z_size)
+    send_side(0, z_here, z_here)
     for distance in straight:
         send_z(distance)
         for k in (distance, z_size - distance):
@@ -359,7 +363,10 @@
     for distance in passed_on:
         wait_z(distance)
         for k in sorted({distance, z_size - distance}):
-            send_x(distance, (z_here + k) % z_size, z_here)
+            z_from = (z_here + k) % z_size
+            send_x(distance, z_from, z_here)
+            if distance not in straight_sides:
+                send_side(distance, z_from, z_here)
     wait_for(rates.at[pl.ds(0, X - 1)], recv_rates.at[1])
 
     def pull(z, x):
@@ -373,35 +380,44 @@
                 value = jnp.concatenate([field_side[x, z], field_side[x_next, z_next]], axis=0)
             rows += [value, pltpu.roll(value, LANES - 1, 1)]
         both = [slot_rows(slots, slot, t) for slot in (0, 1)]
+        values = jnp.concatenate(rows, axis=0)
+        high = values.astype(BF16)
+        low = (values - high.astype(F32)).astype(BF16)
+        one_hot = jnp.concatenate([one_hot_deep(slot[2]) for slot in both], axis=1)
         picked = jnp.dot(
-            split(jnp.concatenate(rows, axis=0)),
-            jnp.concatenate([one_hot_deep(values[2]) for values in both], axis=1),
+            jnp.concatenate([high, low], axis=1),
+            jnp.concatenate([one_hot, one_hot], axis=0),
             preferred_element_type=F32,
         )
-        picked = picked[:80] + picked[80:]
         rate = jnp.concatenate([rates[x, z], jnp.zeros((4, LANES), F32)], axis=0)
         for slot in (0, 1):
             los, sky, deep, f_los, f_sky, f_deep = both[slot]
             at, above = row == los, row == los + 1
-            h_los = jnp.where(at, 1.0 - f_los, 0.0) + jnp.where(above, f_los, 0.0)
-            d_los = jnp.where(above, 1.0, 0.0) - jnp.where(at, 1.0, 0.0)
+            h_los = jnp.where(at, 1.0 - f_los, jnp.where(above, f_los, 0.0))
+            d_los = jnp.where(above, 1.0, jnp.where(at, -1.0, 0.0))
             r_los = jnp.where(at, rate, 0.0)
             at, above = row == sky, row == sky + 1
-            h_sky = jnp.where(at, 1.0 - f_sky, 0.0) + jnp.where(above, f_sky, 0.0)
-            d_sky = jnp.where(above, 1.0, 0.0) - jnp.where(at, 1.0, 0.0)
+            h_sky = jnp.where(at, 1.0 - f_sky, jnp.where(above, f_sky, 0.0))
+            d_sky = jnp.where(above, 1.0, jnp.where(at, -1.0, 0.0))
             lanes = slice(slot * LANES, (slot + 1) * LANES)
-            val, val_sky, val_deep = zero, zero, zero
+            sums = [None] * 3
             for s in range(5):
                 here = picked[s * 16 : s * 16 + 8, lanes]
                 step = picked[s * 16 + 8 : s * 16 + 16, lanes] - here
                 mixed = here + f_deep * step
-                val = val + h_sky[s : s + 1] * mixed
-                val_sky = val_sky + d_sky[s : s + 1] * mixed
-                val_deep = val_deep + h_sky[s : s + 1] * step
-            g_los = jnp.sum(d_los * val, axis=0, keepdims=True)
-            g_sky = jnp.sum(h_los * val_sky, axis=0, keepdims=True)
-            g_deep = jnp.sum(h_los * val_deep, axis=0, keepdims=True)
-            speed = jnp.sum(r_los, axis=0, keepdims=True) * g_los
+                terms = (
+                    h_sky[s : s + 1] * mixed,
+                    d_sky[s : s + 1] * mixed,
+                    h_sky[s : s + 1] * step,
+                )
+                sums = [b if a is None else a + b for a, b in zip(sums, terms, strict=True)]
+            parts = [d_los * sums[0], h_los * sums[1], h_los * sums[2], r_los]
+            parts = [part + pltpu.roll(part, 4, 0) for part in parts]
+            pairs = [jnp.where(row < 4.0, parts[i], parts[i + 1]) for i in (0, 2)]
+            pairs = [pair + pltpu.roll(pair, 2, 0) for pair in pairs]
+            pairs = [pair + pltpu.roll(pair, 1, 0) for pair in pairs]
+            g_los, g_sky = pairs[0][3:4], pairs[0][7:8]
+            g_deep, speed = pairs[1][3:4], pairs[1][7:8] * g_los
             for r, value in enumerate((g_los, g_sky, g_deep, speed)):
                 pulled[slot, r, pl.ds(t, 1), :] = value
 

time: 33.6 us -> 32.7 us (0.973)
  the two profiles are of different devices: /device:TPU:25 before, /device:TPU:2 now
where the time goes in v7:
time: 32.7 us; the launch traced here: 32.5 us
  Pallas kernels  31.9 us (98%)
  between operations  0.64 us (2%)
    pallas_call x1, Pallas kernels, on_device(): pl.pallas_call(kernel, out_shape=(pltpu.VMEM(part_frac.shape, F32), pltpu...  31.2 us

profile of v7, /device:TPU:2, one launch (start us, length us, event | category | flops | bytes accessed | tf_op | source)
XLA Modules:
  0.0 32.5 jit_solution(14841276625514281889)
XLA Ops:
  0.6 31.2 %adjoint.1 = (f32[3,4096]{1,0:T(4,128)S(1)}, f32[32,128]{1,0:T(8,128)S(1)}) custom-call(s32[1,32]{1,0:T(1,128)} %bitcast.5, s32[1,32]{1,0:T(1,128)} %bitcast.6, s32[3,4096]{1,0:T(4,128)} %cell_in.1, f32[3,4096]{1,0:T(4,128)} %frac_in.1, s32[32,128]{1,0:T(8,128)} %bitcast.4, f32[4]{0:T(128)} %bias_in.1, f32[4]{0:T(128)} %rsd_in.1, f32[4,4,128]{2,1,0:T(4,128)} %selection_in.1, ...), custom_call_target="tpu_custom_call" | custom-call | tf_op jit(solution)/shard_map/adjoint/pallas_call | solution.py:492
  31.9 0.7 %write_out.1 = (f32[3,4096]{1,0:T(4,128)}, f32[32,128]{1,0:T(8,128)}) custom-call(f32[3,4096]{1,0:T(4,128)S(1)} %get-tuple-element.6.pos, f32[32,128]{1,0:T(8,128)S(1)} %get-tuple-element.7.vel), custom_call_target="tpu_custom_call" | custom-call | tf_op jit(solution)/shard_map/write_out/pallas_call | solution.py:530

commit v8 on v7

--- a/solution.py
+++ b/solution.py
@@ -230,23 +230,22 @@
     def send_group(step):
         part = pl.ds(step * 2, 2)
         for k in (2, 1, 3, 0):
-            x_to = (x_here + k) % X
-            if k:
-                remote(
-                    grid.at[x_to, part],
-                    rx.at[k - 1, part],
-                    send_sems.at[0],
-                    recv_x.at[step],
-                    x_peer(k),
-                    sky_here,
-                ).start()
             remote(
-                grid_side.at[x_to, part],
+                grid_side.at[(x_here + k) % X, part],
                 rx_side.at[k, part],
                 send_sems.at[0],
                 recv_x.at[step],
                 x_peer(k),
                 sky_up,
+            ).start()
+        for k in (2, 1, 3):
+            remote(
+                grid.at[(x_here + k) % X, part],
+                rx.at[k - 1, part],
+                send_sems.at[0],
+                recv_x.at[step],
+                x_peer(k),
+                sky_here,
             ).start()
 
     def paint_step(step, previous):

time: 32.7 us -> 32.5 us (level)
  no operation moved by 1% of the time
where the time goes in v8:
time: 32.5 us; the launch traced here: 32.4 us
  Pallas kernels  31.7 us (98%)
  between operations  0.64 us (2%)
    pallas_call x1, Pallas kernels, on_device(): pl.pallas_call(kernel, out_shape=(pltpu.VMEM(part_frac.shape, F32), pltpu...  31.1 us
    pallas_call x1, Pallas kernels, on_device(): pl.pallas_call(write_out, out_shape=(jax.ShapeDtypeStruct(grad_pos.shape,...  0.65 us

profile of v8, /device:TPU:2, one launch (start us, length us, event | category | flops | bytes accessed | tf_op | source)
XLA Modules:
  0.0 32.4 jit_solution(13054230490673099019)
XLA Ops:
  0.6 31.1 %adjoint.1 = (f32[3,4096]{1,0:T(4,128)S(1)}, f32[32,128]{1,0:T(8,128)S(1)}) custom-call(s32[1,32]{1,0:T(1,128)} %bitcast.5, s32[1,32]{1,0:T(1,128)} %bitcast.6, s32[3,4096]{1,0:T(4,128)} %cell_in.1, f32[3,4096]{1,0:T(4,128)} %frac_in.1, s32[32,128]{1,0:T(8,128)} %bitcast.4, f32[4]{0:T(128)} %bias_in.1, f32[4]{0:T(128)} %rsd_in.1, f32[4,4,128]{2,1,0:T(4,128)} %selection_in.1, ...), custom_call_target="tpu_custom_call" | custom-call | tf_op jit(solution)/shard_map/adjoint/pallas_call | solution.py:491
  31.7 0.7 %write_out.1 = (f32[3,4096]{1,0:T(4,128)}, f32[32,128]{1,0:T(8,128)}) custom-call(f32[3,4096]{1,0:T(4,128)S(1)} %get-tuple-element.6.pos, f32[32,128]{1,0:T(8,128)S(1)} %get-tuple-element.7.vel), custom_call_target="tpu_custom_call" | custom-call | tf_op jit(solution)/shard_map/write_out/pallas_call | solution.py:529
